TPU v7x, 256 devices: a whole 4x4x8 slice. The times are simulated.
256 devices in a mesh: gx: 8 (over z), gy: 8 (over x, core), gz: 4 (over y).
Axes of the slice: x: 4, y: 4, z: 8, core: 2. Of those that a mesh axis runs over, the one named last changes fastest.
Arguments:
- element_state: float32 [9, 35, 32768], P(None, None, ('gx', 'gy', 'gz')), may hold values from -6 to 6
- jacobians: float32 [3, 9, 9, 32768], P(None, None, None, ('gx', 'gy', 'gz')), may hold values from -1.25 to 1.25
- stiffness: float32 [3, 35, 35], replicated, may hold values from -1 to 1
- projection: float32 [4, 15, 35], replicated, may hold values from -1 to 1
- flux_self: float32 [4, 9, 9, 32768], P(None, None, None, ('gx', 'gy', 'gz')), may hold values from -1 to 1
- flux_other: float32 [4, 9, 9, 32768], P(None, None, None, ('gx', 'gy', 'gz')), may hold values from -1 to 1
- face_source: int32 [4, 32768], P(None, ('gx', 'gy', 'gz')), may hold values from 0 to 607, as said below
- send_faces: int32 [6, 4096], P(None, ('gx', 'gy', 'gz')), may hold values from 0 to 511
- cluster_mask: int32 [32768], P(('gx', 'gy', 'gz')), may hold values from 0 to 1
- seafloor_face: int32 [2097152], P(('gx', 'gy', 'gz')), may hold values from -1 to 511, as said below
- ocean_cell: int32 [64, 4, 8192], P(('gx', 'gy')), may hold values from 0 to 65535
- ocean_weight: float32 [64, 4, 15, 8192], P(('gx', 'gy')), may hold values from 0 to 0.5
- height: float32 [2048, 2048], P('gx', 'gy'), may hold values from -6 to 6
- east_flow: float32 [2048, 2048], P('gx', 'gy'), may hold values from -6 to 6
- north_flow: float32 [2048, 2048], P('gx', 'gy'), may hold values from -6 to 6
- water_depth: float32 [2048, 2048], P('gx', 'gy'), may hold values from 0.5 to 2
Outputs:
- next_state: float32 [9, 35, 32768], P(None, None, ('gx', 'gy', 'gz'))
- new_height: float32 [2048, 2048], P('gx', 'gy')
- new_east: float32 [2048, 2048], P('gx', 'gy')
- new_north: float32 [2048, 2048], P('gx', 'gy')
Inputs may be any that keep to these rules, and one draw needn't show every extreme that they name: `face_source`: within a partition, each of the 96 received columns (numbered from 512) is named by exactly one face; all other faces name the partition's own trace columns. `seafloor_face`: values are local face numbers or -1 for an empty slot. In each block of 128 slots of one partition for one tile the live slots come first and at least one is live; for one tile, the block of every partition is full.
All inputs are finite; a program needn't handle non-finite values.
Results may differ from a plain program's by a relative error of at most 0.0003.
Values sent between devices are 32-bit elements; how exact they have to be, the bound alone decides.
No kernel may reach another device: no remote copies, remote signals or barrier semaphores. Data moves between devices by JAX's collectives and lax.ppermute only.
A program may use at most 128 MiB of HBM per device.

v0:
```python
import jax
import jax.numpy as jnp
from jax import lax
from jax.experimental import pallas as pl
from jax.experimental.pallas import tpu as pltpu
from jax.sharding import PartitionSpec as P

NQ = 9
NB = 35
NF = 15
LN = 128
EL = NQ * LN
TILE = 256
SLAB = 1024
EDGE = EL + TILE

time_step = 1.5
ocean_step = 0.5
f32 = jnp.float32
bf16 = jnp.bfloat16
NT = (((1,), (1,)), ((), ()))


def cost(us):
    return pl.CostEstimate(flops=int(us * 2e8), bytes_accessed=1 << 20, transcendentals=0)


def shaped(*dims):
    return jax.ShapeDtypeStruct(dims, f32)


def split(x):
    high = x.astype(bf16)
    return high, (x - high.astype(f32)).astype(bf16)


def dot3(left, right):
    rows = left.shape[0]
    left_high, left_low = split(left)
    right_high, right_low = split(right)
    both = jnp.dot(
        jnp.concatenate([left_high, left_low], axis=0), right_high, preferred_element_type=f32
    )
    return both[:rows] + both[rows:] + jnp.dot(left_high, right_low, preferred_element_type=f32)


def block(q):
    return pl.ds(q * LN, LN)


def one_hot(row, count, value):
    lanes = row.shape[1]
    target = jnp.broadcast_to(row.astype(f32), (16, lanes)).astype(bf16)
    ids = lax.broadcasted_iota(jnp.int32, (16, lanes), 0).astype(f32)
    zero = jnp.zeros((16, lanes), bf16)
    hits = [target == (ids + 16.0 * c).astype(bf16) for c in range(count // 16)]
    return [jnp.concatenate([jnp.where(h, v, zero) for h in hits], axis=0) for v in value]


def pick(table, index, which, sources):
    found = jnp.zeros(index.shape, f32)
    for s in range(sources):
        taken = jnp.take_along_axis(table(s), index, axis=1)
        found = jnp.where(which == s, taken, found)
    return found


def as_row(column):
    size = column.shape[0]
    eye = lax.broadcasted_iota(jnp.int32, (size, size), 0) == lax.broadcasted_iota(
        jnp.int32, (size, size), 1
    )
    return jnp.sum(jnp.where(eye, column, 0.0), axis=0, keepdims=True)


def as_column(row):
    size = row.shape[1]
    eye = lax.broadcasted_iota(jnp.int32, (size, size), 0) == lax.broadcasted_iota(
        jnp.int32, (size, size), 1
    )
    return jnp.sum(jnp.where(eye, row, 0.0), axis=1, keepdims=True)


def neighbours(x, low_row, high_row):
    size = x.shape[0]
    ids = lax.broadcasted_iota(jnp.int32, x.shape, 0)
    after = jnp.where(ids == size - 1, high_row, pltpu.roll(x, size - 1, 0))
    before = jnp.where(ids == 0, low_row, pltpu.roll(x, 1, 0))
    return after - before


def neighbours_lanes(x, low_col, high_col):
    size = x.shape[1]
    ids = lax.broadcasted_iota(jnp.int32, x.shape, 1)
    after = jnp.where(ids == size - 1, high_col, pltpu.roll(x, size - 1, 1))
    before = jnp.where(ids == 0, low_col, pltpu.roll(x, 1, 1))
    return after - before


def lookup_kernel(meta, weight, cell, height, out, high_low):
    @pl.when(pl.program_id(0) == 0)
    def _():
        high, low = split(height[...])
        high_low[0:TILE] = high
        high_low[TILE:] = low

    layer = meta[0]
    base = pl.program_id(0) * SLAB
    one = jnp.ones((16, TILE), bf16)
    ids = lax.broadcasted_iota(jnp.int32, (TILE, TILE), 0)
    for pair in range(SLAB // TILE):
        start = pl.multiple_of(base + pair * TILE, TILE)
        cells = cell[0, 0:1, pl.ds(start, TILE)]
        for n in range(1, cell.shape[1]):
            cells = jnp.where(layer == n, cell[0, n : n + 1, pl.ds(start, TILE)], cells)
        rows, cols = (cells >> 8, cells & 255)
        (hot,) = one_hot(cols, TILE, [one])
        both = jnp.dot(high_low[...], hot, preferred_element_type=f32)
        found = both[:TILE] + both[TILE:]
        values = jnp.sum(jnp.where(ids == rows, found, 0.0), axis=0, keepdims=True)
        for half in range(2):
            t = 2 * pair + half
            out[t, 0:NF, :] = weight[0, 0, :, t * LN : (t + 1) * LN]
            out[t, NF : NF + 1, :] = values[:, half * LN : (half + 1) * LN]


def lookup(meta, ocean_weight, ocean_cell, height):
    steps = ocean_cell.shape[2] // SLAB
    per = SLAB // LN
    return pl.pallas_call(
        lookup_kernel,
        out_shape=shaped(steps * per, NF + 1, LN),
        grid_spec=pltpu.PrefetchScalarGridSpec(
            num_scalar_prefetch=1,
            grid=(steps,),
            in_specs=[
                pl.BlockSpec((1, 1, NF, SLAB), lambda s, m: (0, m[0], 0, s)),
                pl.BlockSpec(ocean_cell.shape, lambda s, m: (0, 0, 0)),
                pl.BlockSpec(height.shape, lambda s, m: (0, 0)),
            ],
            out_specs=pl.BlockSpec((per, NF + 1, LN), lambda s, m: (s, 0, 0)),
            scratch_shapes=[pltpu.VMEM((2 * TILE, TILE), bf16)],
        ),
        cost_estimate=cost(4),
        name="lookup",
    )(meta, ocean_weight, ocean_cell, height)


def spread_jacobians(jacobians, spread):
    for d in range(3):
        for p in range(NQ):
            for q in range(NQ):
                at = ((d * NQ + p) * NQ + q) * 8
                spread[at : at + 8] = jnp.broadcast_to(jacobians[d, p, q : q + 1, :], (8, LN))


def couple(spread, dof, coupled):
    def rows(b, carry):
        here = pl.ds(pl.multiple_of(b * 8, 8), 8)
        parts = [dof[here, q * LN : (q + 1) * LN] for q in range(NQ)]
        for d in range(3):
            for p in range(NQ):
                total = None
                for q in range(NQ):
                    at = ((d * NQ + p) * NQ + q) * 8
                    term = spread[at : at + 8] * parts[q]
                    total = term if total is None else total + term
                coupled[pl.ds(pl.multiple_of(d * 40 + b * 8, 8), 8), p * LN : (p + 1) * LN] = total
        return carry

    lax.fori_loop(0, 5, rows, 0)


def stiffness_rows(stiffness, pad, transposed):
    total = None
    for d in range(3):
        pad[...] = jnp.zeros((LN, LN), f32)
        pad[0:NB, 0:NB] = stiffness[d]
        value = pad[...].T[0:40] if transposed else pad[0:40]
        value = pltpu.roll(value, d * 40, 1) if d else value
        total = value if total is None else total + value
    return total


def face_rows(projection, pad):
    pad[...] = jnp.zeros((LN, LN), f32)
    for f in range(4):
        pad[f * 16 : f * 16 + NF, 0:NB] = projection[f]
    return pad


def predict_kernel(
    state, jacobians, stiffness, projection, send, east, north, integral, trace, sent,
    spread, dof, coupled, pad, index,
):
    spread_jacobians(jacobians, spread)
    coupled[...] = jnp.zeros((LN, EL), f32)
    dof[...] = jnp.zeros((40, EL), f32)
    for q in range(NQ):
        dof[0:NB, q * LN : (q + 1) * LN] = state[q]
    integral[...] = time_step * dof[...]
    matrix = stiffness_rows(stiffness, pad, False)

    def degree(n, weight):
        couple(spread, dof, coupled)
        current = -dot3(matrix, coupled[...])
        dof[...] = current
        weight = weight * time_step / (n + 2).astype(f32)
        integral[...] = integral[...] + weight * current
        return weight

    lax.fori_loop(0, 4, degree, jnp.float32(time_step))
    faces = face_rows(projection, pad)
    trace[...] = dot3(faces[0:64, 0:40], integral[...])
    index[...] = jnp.zeros((8, LN), jnp.int32)
    index[0:6, 0:16] = send[...]
    lane = lax.broadcasted_iota(jnp.int32, (8, LN), 1)
    wanted = jnp.zeros((8, LN), jnp.int32)
    for spot, direction in enumerate((1, 0, 3, 2, 5, 4)):
        row = jnp.broadcast_to(index[direction : direction + 1, :], (8, LN))
        row = pltpu.roll(row, 16 * spot, 1) if spot else row
        wanted = jnp.where(lane // 16 == spot, row, wanted)
    wanted = jnp.concatenate([wanted, wanted], axis=0)
    for q in range(NQ):
        sent[:, q * LN : (q + 1) * LN] = pick(
            lambda s: trace[s * 16 : (s + 1) * 16, q * LN : (q + 1) * LN],
            wanted & 127, wanted >> 7, 4,
        )
    sent[:, EL:] = jnp.zeros((16, TILE), f32)
    sent[0:1, EL:] = east[0:1, :]
    sent[1:2, EL:] = east[TILE - 1 : TILE, :]
    sent[2:3, EL:] = as_row(north[:, 0:1])
    sent[3:4, EL:] = as_row(north[:, TILE - 1 : TILE])


def predict(state, jacobians, stiffness, projection, send, east, north):
    return pl.pallas_call(
        predict_kernel,
        out_shape=(shaped(40, EL), shaped(64, EL), shaped(16, EDGE)),
        scratch_shapes=[
            pltpu.VMEM((243 * 8, LN), f32),
            pltpu.VMEM((40, EL), f32),
            pltpu.VMEM((LN, EL), f32),
            pltpu.VMEM((LN, LN), f32),
            pltpu.VMEM((8, LN), jnp.int32),
        ],
        cost_estimate=cost(10),
        name="predict",
    )(state, jacobians, stiffness, projection, send, east, north)


def uplift_kernel(inbound, trace, floor, out):
    def tile(r, carry):
        face = jnp.broadcast_to(floor[pl.ds(r, 1), :], (16, LN))
        found = pick(
            lambda s: trace[s * 16 : (s + 1) * 16, 8 * LN : 9 * LN], face & 127, face >> 7, 4
        )
        out[pl.ds(r, 1), :] = jnp.sum(inbound[r] * found, axis=0, keepdims=True)
        return carry

    lax.fori_loop(0, floor.shape[0], tile, 0, unroll=8)


def uplift(inbound, trace, floor):
    return pl.pallas_call(
        uplift_kernel, out_shape=shaped(*floor.shape), cost_estimate=cost(2), name="uplift"
    )(inbound, trace, floor)


def volume_kernel(
    state, jacobians, stiffness, integral, inbound, floor, base, load, spread, coupled, pad, left, right
):
    spread_jacobians(jacobians, spread)
    coupled[...] = jnp.zeros((LN, EL), f32)
    couple(spread, integral, coupled)
    volume = dot3(stiffness_rows(stiffness, pad, True), coupled[...])
    base[...] = volume
    for q in range(NQ):
        here = pl.ds(q * LN, LN)
        base[0:NB, here] = volume[0:NB, q * LN : (q + 1) * LN] + state[q]
    zero = jnp.zeros((16, LN), bf16)
    one = jnp.ones((16, LN), bf16)

    def chunk(c, total):
        for i in range(8):
            r = c * 8 + i
            lanes = slice(i * LN, (i + 1) * LN)
            face = floor[pl.ds(r, 1), :]
            part = inbound[r]
            high, low = split(part * part[NF : NF + 1, :])
            (hot,) = one_hot(face & 127, LN, [one])
            right[:, lanes] = hot
            side = jnp.broadcast_to((face >> 7).astype(f32), (16, LN)).astype(bf16)
            for f in range(4):
                hit = side == jnp.full((16, LN), f, bf16)
                left[f * 16 : (f + 1) * 16, lanes] = jnp.where(hit, high, zero)
                left[64 + f * 16 : 64 + (f + 1) * 16, lanes] = jnp.where(hit, low, zero)
        return total + lax.dot_general(left[...], right[...], NT, preferred_element_type=f32)

    total = lax.fori_loop(0, floor.shape[0] // 8, chunk, jnp.zeros((LN, LN), f32))
    load[...] = total[:64] + total[64:]


def volume(state, jacobians, stiffness, integral, inbound, floor):
    return pl.pallas_call(
        volume_kernel,
        out_shape=(shaped(40, EL), shaped(64, LN)),
        scratch_shapes=[
            pltpu.VMEM((243 * 8, LN), f32),
            pltpu.VMEM((LN, EL), f32),
            pltpu.VMEM((LN, LN), f32),
            pltpu.VMEM((LN, SLAB), bf16),
            pltpu.VMEM((LN, SLAB), bf16),
        ],
        cost_estimate=cost(6),
        name="volume",
    )(state, jacobians, stiffness, integral, inbound, floor)


def flux_kernel(
    meta, state, base, load, trace, below_x, above_x, below_y, above_y, below_z, above_z,
    source, own, other, projection, mask, out, numeric, received, pad,
):
    faces = face_rows(projection, pad)
    matrix = faces[...].T[0:40, 0:64]
    lane = lax.broadcasted_iota(jnp.int32, (16, LN), 1)
    sides = (
        (below_x, meta[1] > 0), (above_x, meta[1] < meta[4] - 1),
        (below_y, meta[2] > 0), (above_y, meta[2] < meta[5] - 1),
        (below_z, meta[0] > 0), (above_z, meta[0] < meta[3] - 1),
    )
    low = [jnp.where(there, 16 * n, LN) for n, (_, there) in enumerate(sides)]
    for q in range(NQ):
        here = slice(q * LN, (q + 1) * LN)
        found = jnp.zeros((16, LN), f32)
        for n, (side, _) in enumerate(sides):
            hit = (lane >= low[n]) & (lane < low[n] + 16)
            found = jnp.where(hit, side[:, here], found)
        received[:, here] = found

    def face(f, carry):
        which = jnp.broadcast_to(source[pl.ds(f, 1), :], (16, LN))
        rows = pl.ds(pl.multiple_of(f * 16, 16), 16)
        total = [None] * NQ
        for q in range(NQ):
            here = slice(q * LN, (q + 1) * LN)
            mine = trace[rows, here]
            remote = pick(
                lambda s: received[:, here] if s == 4 else trace[s * 16 : (s + 1) * 16, here],
                which & 127, which >> 7, 5,
            )
            for p in range(NQ):
                term = mine * own[f, q, p : p + 1, :] + remote * other[f, q, p : p + 1, :]
                total[p] = term if total[p] is None else total[p] + term
        for p in range(NQ):
            numeric[rows, p * LN : (p + 1) * LN] = total[p]
        return carry

    lax.fori_loop(0, 4, face, 0)
    numeric[:, 2 * LN : 3 * LN] = numeric[:, 2 * LN : 3 * LN] + load[...]
    taken = dot3(matrix, numeric[...])
    updated = base[...] - taken
    live = mask[...] > 0
    for p in range(NQ):
        out[p] = jnp.where(live, updated[0:NB, p * LN : (p + 1) * LN], state[p])


def flux(meta, state, base, load, trace, received, source, own, other, projection, mask):
    smem = pl.BlockSpec(memory_space=pltpu.SMEM)
    vmem = pl.BlockSpec(memory_space=pltpu.VMEM)
    return pl.pallas_call(
        flux_kernel,
        out_shape=shaped(NQ, NB, LN),
        in_specs=[smem] + [vmem] * 15,
        out_specs=vmem,
        scratch_shapes=[
            pltpu.VMEM((64, EL), f32),
            pltpu.VMEM((16, EL), f32),
            pltpu.VMEM((LN, LN), f32),
        ],
        cost_estimate=cost(6),
        name="flux",
    )(meta, state, base, load, trace, *received, source, own, other, projection, mask)


def ocean_kernel(
    meta, first, second, third, fourth, cell, below_x, above_x, below_y, above_y,
    height, east, north, depth, new_height, edges, left, right, total, lifts,
):
    layers = meta[3]
    per = first.shape[0]
    total[...] = jnp.zeros((2 * TILE, TILE), f32)
    one = jnp.ones((16, LN), bf16)
    for shift, values in enumerate((first, second, third, fourth)):
        layer = lax.rem(meta[0] - shift + layers, layers)
        lifts[pl.ds(pl.multiple_of(layer * per, 8), per)] = values[...]
    for layer in range(4):

        def chunk(c, carry):
            for i in range(8):
                r = c * 8 + i
                lanes = slice(i * LN, (i + 1) * LN)
                start = pl.multiple_of(r * LN, LN)
                cells = cell[0, layer : layer + 1, pl.ds(start, LN)]
                value = jnp.broadcast_to(lifts[pl.ds(layer * per + r, 1), :], (16, LN))
                high, low = one_hot(cells >> 8, TILE, split(value))
                left[0:TILE, lanes] = high
                left[TILE:, lanes] = low
                (right[:, lanes],) = one_hot(cells & 255, TILE, [one])
            total[...] += lax.dot_general(
                left[...], right[...], NT, preferred_element_type=f32
            )
            return carry

        lax.fori_loop(0, per // 8, chunk, 0)
    source = total[0:TILE] + total[TILE:]
    rim = slice(EL, EDGE)
    low_x = jnp.where(meta[1] > 0, below_x[1:2, rim], 0.0)
    high_x = jnp.where(meta[1] < meta[4] - 1, above_x[0:1, rim], 0.0)
    low_y = as_column(jnp.where(meta[2] > 0, below_y[3:4, rim], 0.0))
    high_y = as_column(jnp.where(meta[2] < meta[5] - 1, above_y[2:3, rim], 0.0))
    slope = neighbours(east[...], low_x, high_x) * 0.5
    slope = slope + neighbours_lanes(north[...], low_y, high_y) * 0.5
    updated = height[...] + ocean_step * (source - depth[...] * slope)
    new_height[...] = updated
    edges[...] = jnp.zeros((8, TILE), f32)
    edges[0:1] = updated[0:1, :]
    edges[1:2] = updated[TILE - 1 : TILE, :]
    edges[2:3] = as_row(updated[:, 0:1])
    edges[3:4] = as_row(updated[:, TILE - 1 : TILE])


def ocean(meta, layers, cell, received, height, east, north, depth):
    smem = pl.BlockSpec(memory_space=pltpu.SMEM)
    vmem = pl.BlockSpec(memory_space=pltpu.VMEM)
    return pl.pallas_call(
        ocean_kernel,
        out_shape=(shaped(TILE, TILE), shaped(8, TILE)),
        in_specs=[smem] + [vmem] * 13,
        out_specs=(vmem, vmem),
        scratch_shapes=[
            pltpu.VMEM((2 * TILE, SLAB), bf16),
            pltpu.VMEM((TILE, SLAB), bf16),
            pltpu.VMEM((2 * TILE, TILE), f32),
            pltpu.VMEM((4 * layers[0].shape[0], LN), f32),
        ],
        cost_estimate=cost(10),
        name="ocean",
    )(meta, *layers, cell, *received[:4], height, east, north, depth)


def flow_kernel(meta, height, east, north, below_x, above_x, below_y, above_y, new_east, new_north):
    low_x = jnp.where(meta[1] > 0, below_x[1:2], 0.0)
    high_x = jnp.where(meta[1] < meta[4] - 1, above_x[0:1], 0.0)
    low_y = as_column(jnp.where(meta[2] > 0, below_y[3:4], 0.0))
    high_y = as_column(jnp.where(meta[2] < meta[5] - 1, above_y[2:3], 0.0))
    level = height[...]
    new_east[...] = east[...] - ocean_step * neighbours(level, low_x, high_x) * 0.5
    new_north[...] = north[...] - ocean_step * neighbours_lanes(level, low_y, high_y) * 0.5


def flow(meta, height, east, north, received):
    smem = pl.BlockSpec(memory_space=pltpu.SMEM)
    vmem = pl.BlockSpec(memory_space=pltpu.VMEM)
    return pl.pallas_call(
        flow_kernel,
        out_shape=(shaped(TILE, TILE), shaped(TILE, TILE)),
        in_specs=[smem] + [vmem] * 7,
        out_specs=(vmem, vmem),
        cost_estimate=cost(2),
        name="flow",
    )(meta, height, east, north, *received)


def shifted(value, axis, step):
    count = lax.axis_size(axis)
    return lax.ppermute(value, axis, [(i, (i + step) % count) for i in range(count)])


def on_device(
    element_state,
    jacobians,
    stiffness,
    projection,
    flux_self,
    flux_other,
    face_source,
    send_faces,
    cluster_mask,
    seafloor_face,
    ocean_cell,
    ocean_weight,
    height,
    east_flow,
    north_flow,
    water_depth,
):
    names = ("gz", "gx", "gy")
    spot = jnp.arange(8, dtype=jnp.int32)
    meta = jnp.zeros((8,), jnp.int32)
    for n, axis in enumerate(names):
        meta = jnp.where(spot == n, lax.axis_index(axis).astype(jnp.int32), meta)
        meta = jnp.where(spot == n + 3, lax.axis_size(axis), meta)
    floor = seafloor_face.reshape(-1, LN)
    mask = cluster_mask.reshape(1, LN)
    outbound = lookup(meta, ocean_weight, ocean_cell, height)
    inbound = lax.all_to_all(outbound, ("gx", "gy"), 0, 0, tiled=True)
    integral, trace, sent = predict(
        element_state, jacobians, stiffness, projection, send_faces, east_flow, north_flow
    )
    lifted = uplift(inbound, trace, floor)
    landed = lax.all_to_all(lifted, ("gx", "gy"), 0, 0, tiled=True)
    received = [shifted(sent, axis, step) for axis in ("gx", "gy", "gz") for step in (1, -1)]
    layers = [landed] + [shifted(landed, "gz", step) for step in (1, 2, 3)]
    base, load = volume(element_state, jacobians, stiffness, integral, inbound, floor)
    new_height, edges = ocean(
        meta, layers, ocean_cell, received, height, east_flow, north_flow, water_depth
    )
    rims = [shifted(edges, axis, step) for axis in ("gx", "gy") for step in (1, -1)]
    next_state = flux(
        meta, element_state, base, load, trace, received, face_source, flux_self, flux_other,
        projection, mask,
    )
    new_east, new_north = flow(meta, new_height, east_flow, north_flow, rims)
    return (next_state, new_height, new_east, new_north)


def solution(mesh):
    return jax.shard_map(
        on_device,
        mesh=mesh,
        in_specs=(
            P(None, None, ("gx", "gy", "gz")),
            P(None, None, None, ("gx", "gy", "gz")),
            P(),
            P(),
            P(None, None, None, ("gx", "gy", "gz")),
            P(None, None, None, ("gx", "gy", "gz")),
            P(None, ("gx", "gy", "gz")),
            P(None, ("gx", "gy", "gz")),
            P(("gx", "gy", "gz")),
            P(("gx", "gy", "gz")),
            P(("gx", "gy"), None, None),
            P(("gx", "gy"), None, None, None),
            P("gx", "gy"),
            P("gx", "gy"),
            P("gx", "gy"),
            P("gx", "gy"),
        ),
        out_specs=(P(None, None, ("gx", "gy", "gz")), P("gx", "gy"), P("gx", "gy"), P("gx", "gy")),
        check_vma=False,
    )
```

profile of v0, /device:TPU:7, one launch (start us, length us, event | category | flops | bytes accessed | tf_op | source)
XLA Modules:
  0.0 106.9 jit_solution(5848691491330421159)
XLA Ops:
  0.6 4.1 %copy.29.weight = f32[1,4,15,8192]{3,2,1,0:T(8,128)} copy(f32[1,4,15,8192]{3,1,2,0:T(4,128)} %param.27) | data formatting | bytes 3932160 | tf_op args[11]
  5.2 7.6 %lookup.1 = f32[64,16,128]{2,1,0:T(8,128)} custom-call(s32[8]{0:T(128)} %compare_select_fusion.5.meta, f32[1,4,15,8192]{3,2,1,0:T(8,128)} %copy.29.weight, s32[1,4,8192]{2,1,0:T(4,128)} %cell.3, f32[256,256]{1,0:T(8,128)} %height.3), custom_call_target="tpu_custom_call" | custom-call | flops 800000000 | bytes 1048576 | tf_op jit(solution)/shard_map/lookup/pallas_call | solution.py:130
  12.8 12.2 %all-to-all-start = ((f32[64,16,128]{2,1,0:T(8,128)}), f32[64,16,128]{2,1,0:T(8,128)S(1)}, u32[]{:S(2)}, u32[]{:S(2)}) async-start(f32[64,16,128]{2,1,0:T(8,128)} %lookup.1), calls=%async_computation | async-start | bytes 1048576 | tf_op jit(solution)/shard_map/all_to_all | solution.py:507
  25.1 0.7 copy.30.jacobians
  26.4 5.0 %predict.1 = (f32[40,1152]{1,0:T(8,128)}, f32[64,1152]{1,0:T(8,128)}, f32[16,1408]{1,0:T(8,128)}) custom-call(f32[9,35,128]{2,1,0:T(8,128)} %state.5, f32[3,9,9,128]{3,2,1,0:T(8,128)} %copy.30.jacobians, f32[3,35,35]{2,1,0:T(8,128)} %stiffness.3, f32[4,15,35]{2,1,0:T(8,128)} %copy.28.projection, s32[6,16]{1,0:T(8,128)} %send.1, f32[256,256]{1,0:T(8,128)} %east.5, ...), custom_call_target="tpu_custom_call" | custom-call | flops 2000000000 | bytes 1048576 | tf_op jit(solution)/shard_map/predict/pallas_call | solution.py:237
  31.4 1.2 %collective-permute-start = (f32[16,1408]{1,0:T(8,128)}, f32[16,1408]{1,0:T(8,128)S(1)}, u32[]{:S(2)}, u32[]{:S(2)}) collective-permute-start(f32[16,1408]{1,0:T(8,128)} %get-tuple-element.17), channel_id=1, source_target_pairs={{0,32},{32,64},{64,96},{96,128},{128,160},{160,192},{192,224},{224... | collective-permute-start | bytes 270344 | tf_op jit(solution)/shard_map/ppermute | solution.py:477
  32.6 1.6 %collective-permute-start.1 = (f32[16,1408]{1,0:T(8,128)}, f32[16,1408]{1,0:T(8,128)S(1)}, u32[]{:S(2)}, u32[]{:S(2)}) collective-permute-start(f32[16,1408]{1,0:T(8,128)} %get-tuple-element.17), channel_id=1, source_target_pairs={{0,224},{32,0},{64,32},{96,64},{128,96},{160,128},{192,160},{224,1... | collective-permute-start | bytes 270344 | tf_op jit(solution)/shard_map/ppermute | solution.py:477
  34.2 7.1 %all-to-all-done.inbound = f32[64,16,128]{2,1,0:T(8,128)S(1)} async-done(((f32[64,16,128]{2,1,0:T(8,128)}), f32[64,16,128]{2,1,0:T(8,128)S(1)}, u32[]{:S(2)}, u32[]{:S(2)}) %all-to-all-start) | async-done | bytes 524320 | tf_op jit(solution)/shard_map/all_to_all | solution.py:507
  41.4 0.8 copy-done
  42.2 3.3 %uplift.1 = f32[64,128]{1,0:T(8,128)} custom-call(f32[64,16,128]{2,1,0:T(8,128)} %copy-done, f32[64,1152]{1,0:T(8,128)} %get-tuple-element.16.trace, s32[64,128]{1,0:T(8,128)} %bitcast.11), custom_call_target="tpu_custom_call" | custom-call | flops 400000000 | bytes 1048576 | tf_op jit(solution)/shard_map/uplift/pallas_call | solution.py:265
  45.5 7.4 %all-to-all-start.1 = ((f32[64,1,128]{2,1,0:T(1,128)}), f32[64,1,128]{2,1,0:T(1,128)S(1)}, u32[]{:S(2)}, u32[]{:S(2)}) async-start(f32[64,1,128]{2,1,0:T(1,128)} %bitcast.10), calls=%async_computation.1 | async-start | bytes 65536 | tf_op jit(solution)/shard_map/all_to_all | solution.py:512
  53.4 0.8 copy.31.own
  54.1 0.8 copy.32.other
  54.9 5.5 %all-to-all-done.1 = f32[64,1,128]{2,1,0:T(1,128)S(1)} async-done(((f32[64,1,128]{2,1,0:T(1,128)}), f32[64,1,128]{2,1,0:T(1,128)S(1)}, u32[]{:S(2)}, u32[]{:S(2)}) %all-to-all-start.1) | async-done | bytes 32800 | tf_op jit(solution)/shard_map/all_to_all | solution.py:512
  60.4 1.3 %collective-permute-start.6 = (f32[64,128]{1,0:T(8,128)S(1)}, f32[64,128]{1,0:T(8,128)S(1)}, u32[]{:S(2)}, u32[]{:S(2)}) collective-permute-start(f32[64,128]{1,0:T(8,128)S(1)} %bitcast.6), channel_id=1, source_target_pairs={{0,1},{1,2},{2,3},{3,0},{4,5},{5,6},{6,7},{7,4},{8,9},{9,10},{10,1... | collective-permute-start | bytes 98312 | tf_op jit(solution)/shard_map/ppermute | solution.py:477
  61.7 2.6 %collective-permute-start.7 = (f32[64,128]{1,0:T(8,128)S(1)}, f32[64,128]{1,0:T(8,128)S(1)}, u32[]{:S(2)}, u32[]{:S(2)}) collective-permute-start(f32[64,128]{1,0:T(8,128)S(1)} %bitcast.7), channel_id=1, source_target_pairs={{0,2},{1,3},{2,0},{3,1},{4,6},{5,7},{6,4},{7,5},{8,10},{9,11},{10,... | collective-permute-start | bytes 98312 | tf_op jit(solution)/shard_map/ppermute | solution.py:477
  64.4 1.1 collective-permute-start.8
  65.4 5.2 %volume.1 = (f32[40,1152]{1,0:T(8,128)}, f32[64,128]{1,0:T(8,128)}) custom-call(f32[9,35,128]{2,1,0:T(8,128)} %state.5, f32[3,9,9,128]{3,2,1,0:T(8,128)} %copy.30.jacobians, f32[3,35,35]{2,1,0:T(8,128)} %stiffness.3, f32[40,1152]{1,0:T(8,128)} %get-tuple-element.13.integral, f32[64,16,128]{2,1,0:T(8,128)} %copy-done, s32[64,128]{1,0:T(8,128)} %bitcast.12), custom_call_target="tpu_custom_call" | custom-call | flops 1200000000 | bytes 1048576 | tf_op jit(solution)/shard_map/volume/pallas_call | solution.py:305
  71.2 2.3 %collective-permute-start.5 = (f32[16,1408]{1,0:T(8,128)S(1)}, f32[16,1408]{1,0:T(8,128)S(1)}, u32[]{:S(2)}, u32[]{:S(2)}) collective-permute-start(f32[16,1408]{1,0:T(8,128)S(1)} %copy-done.7), channel_id=1, source_target_pairs={{0,3},{1,0},{2,1},{3,2},{4,7},{5,4},{6,5},{7,6},{8,11},{9,8},{10,9... | collective-permute-start | bytes 270344 | tf_op jit(solution)/shard_map/ppermute | solution.py:477
  74.7 19.8 %ocean.1 = (f32[256,256]{1,0:T(8,128)}, f32[8,256]{1,0:T(8,128)}) custom-call(s32[8]{0:T(128)} %compare_select_fusion.5.meta, f32[64,128]{1,0:T(8,128)} %bitcast.9, f32[64,128]{1,0:T(8,128)} %copy-done.13, f32[64,128]{1,0:T(8,128)} %copy-done.14, f32[64,128]{1,0:T(8,128)} %copy-done.15, s32[1,4,8192]{2,1,0:T(4,128)} %cell.3, f32[16,1408]{1,0:T(8,128)} %copy-done.6, ...), custom_call_target="tpu_custom_call" | custom-call | flops 2000000000 | bytes 1048576 | tf_op jit(solution)/shard_map/ocean/pallas_call | solution.py:436
  95.0 3.8 %collective-permute-start.11 = (f32[8,256]{1,0:T(8,128)}, f32[8,256]{1,0:T(8,128)S(1)}, u32[]{:S(2)}, u32[]{:S(2)}) collective-permute-start(f32[8,256]{1,0:T(8,128)} %get-tuple-element.19), channel_id=1, source_target_pairs={{0,4},{4,8},{8,12},{12,16},{16,20},{20,24},{24,28},{28,0},{1,5},{5... | collective-permute-start | bytes 24584 | tf_op jit(solution)/shard_map/ppermute | solution.py:477
  98.8 1.3 %collective-permute-start.9 = (f32[8,256]{1,0:T(8,128)}, f32[8,256]{1,0:T(8,128)S(1)}, u32[]{:S(2)}, u32[]{:S(2)}) collective-permute-start(f32[8,256]{1,0:T(8,128)} %get-tuple-element.19), channel_id=1, source_target_pairs={{0,32},{32,64},{64,96},{96,128},{128,160},{160,192},{192,224},{224... | collective-permute-start | bytes 24584 | tf_op jit(solution)/shard_map/ppermute | solution.py:477
  100.8 3.3 %flux.1 = f32[9,35,128]{2,1,0:T(8,128)} custom-call(s32[8]{0:T(128)} %compare_select_fusion.5.meta, f32[9,35,128]{2,1,0:T(8,128)} %state.5, f32[40,1152]{1,0:T(8,128)} %get-tuple-element.14.base, f32[64,128]{1,0:T(8,128)} %get-tuple-element.15.load, f32[64,1152]{1,0:T(8,128)} %get-tuple-element.16.trace, f32[16,1408]{1,0:T(8,128)} %copy-done.6, ...), custom_call_target="tpu_custom_call" | custom-call | flops 1200000000 | bytes 1048576 | tf_op jit(solution)/shard_map/flux/pallas_call | solution.py:371
  104.7 2.2 %flow.1 = (f32[256,256]{1,0:T(8,128)}, f32[256,256]{1,0:T(8,128)}) custom-call(s32[8]{0:T(128)} %compare_select_fusion.5.meta, f32[256,256]{1,0:T(8,128)} %get-tuple-element.10.height, f32[256,256]{1,0:T(8,128)} %east.5, f32[256,256]{1,0:T(8,128)} %north.5, f32[8,256]{1,0:T(8,128)} %copy-done.19, f32[8,256]{1,0:T(8,128)} %copy-done.16, f32[8,256]{1,0:T(8,128)} %copy-done.17, ...), custom_call_target="tpu_custom_call" | custom-call | flops 400000000 | bytes 1048576 | tf_op jit(solution)/shard_map/flow/pallas_call | solution.py:465
  (59 shorter events, 5.1 us)
Async XLA Ops:
  4.7 20.4 %copy-start.3 = (f32[3,9,9,128]{3,0,2,1:T(4,128)S(1)}, f32[3,9,9,128]{3,0,2,1:T(4,128)}, u32[]{:S(2)}) copy-start(f32[3,9,9,128]{3,0,2,1:T(4,128)} %param.17) | copy-start | bytes 373252
  5.2 20.6 %copy-start.5 = (f32[4,15,35]{2,0,1:T(4,128)S(1)}, f32[4,15,35]{2,0,1:T(4,128)}, u32[]{:S(2)}) copy-start(f32[4,15,35]{2,0,1:T(4,128)} %param.19) | copy-start | bytes 25204
  12.8 28.5 %all-to-all-start = ((f32[64,16,128]{2,1,0:T(8,128)}), f32[64,16,128]{2,1,0:T(8,128)S(1)}, u32[]{:S(2)}, u32[]{:S(2)}) async-start(f32[64,16,128]{2,1,0:T(8,128)} %lookup.1), calls=%async_computation | async-start | bytes 1048576 | tf_op jit(solution)/shard_map/all_to_all | solution.py:507
  26.4 27.0 %copy-start.1 = (f32[4,9,9,128]{3,0,2,1:T(4,128)S(1)}, f32[4,9,9,128]{3,0,2,1:T(4,128)}, u32[]{:S(2)}) copy-start(f32[4,9,9,128]{3,0,2,1:T(4,128)} %param.20) | copy-start | bytes 497668
  31.4 22.7 %copy-start.2 = (f32[4,9,9,128]{3,0,2,1:T(4,128)S(1)}, f32[4,9,9,128]{3,0,2,1:T(4,128)}, u32[]{:S(2)}) copy-start(f32[4,9,9,128]{3,0,2,1:T(4,128)} %param.21) | copy-start | bytes 497668
  31.4 30.3 %collective-permute-start = (f32[16,1408]{1,0:T(8,128)}, f32[16,1408]{1,0:T(8,128)S(1)}, u32[]{:S(2)}, u32[]{:S(2)}) collective-permute-start(f32[16,1408]{1,0:T(8,128)} %get-tuple-element.17), channel_id=1, source_target_pairs={{0,32},{32,64},{64,96},{96,128},{128,160},{160,192},{192,224},{224... | collective-permute-start | bytes 270344 | tf_op jit(solution)/shard_map/ppermute | solution.py:477
  32.6 31.7 %collective-permute-start.1 = (f32[16,1408]{1,0:T(8,128)}, f32[16,1408]{1,0:T(8,128)S(1)}, u32[]{:S(2)}, u32[]{:S(2)}) collective-permute-start(f32[16,1408]{1,0:T(8,128)} %get-tuple-element.17), channel_id=1, source_target_pairs={{0,224},{32,0},{64,32},{96,64},{128,96},{160,128},{192,160},{224,1... | collective-permute-start | bytes 270344 | tf_op jit(solution)/shard_map/ppermute | solution.py:477
  45.5 15.0 %all-to-all-start.1 = ((f32[64,1,128]{2,1,0:T(1,128)}), f32[64,1,128]{2,1,0:T(1,128)S(1)}, u32[]{:S(2)}, u32[]{:S(2)}) async-start(f32[64,1,128]{2,1,0:T(1,128)} %bitcast.10), calls=%async_computation.1 | async-start | bytes 65536 | tf_op jit(solution)/shard_map/all_to_all | solution.py:512
  52.9 17.8 %collective-permute-start.2 = (f32[16,1408]{1,0:T(8,128)}, f32[16,1408]{1,0:T(8,128)S(1)}, u32[]{:S(2)}, u32[]{:S(2)}) collective-permute-start(f32[16,1408]{1,0:T(8,128)} %get-tuple-element.17), channel_id=1, source_target_pairs={{0,4},{4,8},{8,12},{12,16},{16,20},{20,24},{24,28},{28,0},{1,5},{5... | collective-permute-start | bytes 270344 | tf_op jit(solution)/shard_map/ppermute | solution.py:477
  53.3 17.9 %collective-permute-start.3 = (f32[16,1408]{1,0:T(8,128)}, f32[16,1408]{1,0:T(8,128)S(1)}, u32[]{:S(2)}, u32[]{:S(2)}) collective-permute-start(f32[16,1408]{1,0:T(8,128)} %get-tuple-element.17), channel_id=1, source_target_pairs={{0,28},{4,0},{8,4},{12,8},{16,12},{20,16},{24,20},{28,24},{1,29},{... | collective-permute-start | bytes 270344 | tf_op jit(solution)/shard_map/ppermute | solution.py:477
  60.4 10.2 %copy-start.4 = (f32[64,1,128]{2,1,0:T(1,128)}, f32[64,1,128]{2,1,0:T(1,128)S(1)}, u32[]{:S(2)}) copy-start(f32[64,1,128]{2,1,0:T(1,128)S(1)} %all-to-all-done.1) | copy-start | bytes 98308
  60.4 13.0 %collective-permute-start.6 = (f32[64,128]{1,0:T(8,128)S(1)}, f32[64,128]{1,0:T(8,128)S(1)}, u32[]{:S(2)}, u32[]{:S(2)}) collective-permute-start(f32[64,128]{1,0:T(8,128)S(1)} %bitcast.6), channel_id=1, source_target_pairs={{0,1},{1,2},{2,3},{3,0},{4,5},{5,6},{6,7},{7,4},{8,9},{9,10},{10,1... | collective-permute-start | bytes 98312 | tf_op jit(solution)/shard_map/ppermute | solution.py:477
  61.7 8.9 %copy-start.6 = (f32[16,1408]{1,0:T(8,128)}, f32[16,1408]{1,0:T(8,128)S(1)}, u32[]{:S(2)}) copy-start(f32[16,1408]{1,0:T(8,128)S(1)} %collective-permute-done.below_x) | copy-start | bytes 270340
  61.7 11.7 %collective-permute-start.7 = (f32[64,128]{1,0:T(8,128)S(1)}, f32[64,128]{1,0:T(8,128)S(1)}, u32[]{:S(2)}, u32[]{:S(2)}) collective-permute-start(f32[64,128]{1,0:T(8,128)S(1)} %bitcast.7), channel_id=1, source_target_pairs={{0,2},{1,3},{2,0},{3,1},{4,6},{5,7},{6,4},{7,5},{8,10},{9,11},{10,... | collective-permute-start | bytes 98312 | tf_op jit(solution)/shard_map/ppermute | solution.py:477
  64.4 6.3 %copy-start.8 = (f32[16,1408]{1,0:T(8,128)}, f32[16,1408]{1,0:T(8,128)S(1)}, u32[]{:S(2)}) copy-start(f32[16,1408]{1,0:T(8,128)S(1)} %collective-permute-done.1.above_x) | copy-start | bytes 270340
  64.4 9.1 %collective-permute-start.8 = (f32[64,128]{1,0:T(8,128)S(1)}, f32[64,128]{1,0:T(8,128)S(1)}, u32[]{:S(2)}, u32[]{:S(2)}) collective-permute-start(f32[64,128]{1,0:T(8,128)S(1)} %bitcast.8), channel_id=1, source_target_pairs={{0,3},{1,0},{2,1},{3,2},{4,7},{5,4},{6,5},{7,6},{8,11},{9,8},{10,9... | collective-permute-start | bytes 98312 | tf_op jit(solution)/shard_map/ppermute | solution.py:477
  65.4 5.3 %copy-start.7 = (f32[16,1408]{1,0:T(8,128)S(1)}, f32[16,1408]{1,0:T(8,128)}, u32[]{:S(2)}) copy-start(f32[16,1408]{1,0:T(8,128)} %get-tuple-element.17) | copy-start | bytes 270340
  70.7 2.8 %copy-start.9 = (f32[16,1408]{1,0:T(8,128)}, f32[16,1408]{1,0:T(8,128)S(1)}, u32[]{:S(2)}) copy-start(f32[16,1408]{1,0:T(8,128)S(1)} %collective-permute-done.2.below_y) | copy-start | bytes 270340
  70.7 28.1 %collective-permute-start.4 = (f32[16,1408]{1,0:T(8,128)S(1)}, f32[16,1408]{1,0:T(8,128)S(1)}, u32[]{:S(2)}, u32[]{:S(2)}) collective-permute-start(f32[16,1408]{1,0:T(8,128)S(1)} %copy-done.7), channel_id=1, source_target_pairs={{0,1},{1,2},{2,3},{3,0},{4,5},{5,6},{6,7},{7,4},{8,9},{9,10},{10,1... | collective-permute-start | bytes 270344 | tf_op jit(solution)/shard_map/ppermute | solution.py:477
  71.2 29.0 %collective-permute-start.5 = (f32[16,1408]{1,0:T(8,128)S(1)}, f32[16,1408]{1,0:T(8,128)S(1)}, u32[]{:S(2)}, u32[]{:S(2)}) collective-permute-start(f32[16,1408]{1,0:T(8,128)S(1)} %copy-done.7), channel_id=1, source_target_pairs={{0,3},{1,0},{2,1},{3,2},{4,7},{5,4},{6,5},{7,6},{8,11},{9,8},{10,9... | collective-permute-start | bytes 270344 | tf_op jit(solution)/shard_map/ppermute | solution.py:477
  94.5 9.6 %collective-permute-start.10 = (f32[8,256]{1,0:T(8,128)}, f32[8,256]{1,0:T(8,128)S(1)}, u32[]{:S(2)}, u32[]{:S(2)}) collective-permute-start(f32[8,256]{1,0:T(8,128)} %get-tuple-element.19), channel_id=1, source_target_pairs={{0,224},{32,0},{64,32},{96,64},{128,96},{160,128},{192,160},{224,1... | collective-permute-start | bytes 24584 | tf_op jit(solution)/shard_map/ppermute | solution.py:477
  95.0 9.1 %collective-permute-start.11 = (f32[8,256]{1,0:T(8,128)}, f32[8,256]{1,0:T(8,128)S(1)}, u32[]{:S(2)}, u32[]{:S(2)}) collective-permute-start(f32[8,256]{1,0:T(8,128)} %get-tuple-element.19), channel_id=1, source_target_pairs={{0,4},{4,8},{8,12},{12,16},{16,20},{20,24},{24,28},{28,0},{1,5},{5... | collective-permute-start | bytes 24584 | tf_op jit(solution)/shard_map/ppermute | solution.py:477
  98.8 5.3 %collective-permute-start.12 = (f32[8,256]{1,0:T(8,128)}, f32[8,256]{1,0:T(8,128)S(1)}, u32[]{:S(2)}, u32[]{:S(2)}) collective-permute-start(f32[8,256]{1,0:T(8,128)} %get-tuple-element.19), channel_id=1, source_target_pairs={{0,28},{4,0},{8,4},{12,8},{16,12},{20,16},{24,20},{28,24},{1,29},{... | collective-permute-start | bytes 24584 | tf_op jit(solution)/shard_map/ppermute | solution.py:477
  98.8 5.3 %collective-permute-start.9 = (f32[8,256]{1,0:T(8,128)}, f32[8,256]{1,0:T(8,128)S(1)}, u32[]{:S(2)}, u32[]{:S(2)}) collective-permute-start(f32[8,256]{1,0:T(8,128)} %get-tuple-element.19), channel_id=1, source_target_pairs={{0,32},{32,64},{64,96},{96,128},{128,160},{160,192},{192,224},{224... | collective-permute-start | bytes 24584 | tf_op jit(solution)/shard_map/ppermute | solution.py:477
  (11 other events, 9.3 us)
where the time goes:
time: 109 us; the launch traced here: 107 us
  Pallas kernels  46.4 us (43%)
  starting transfers between devices  36.3 us (33%)
  waiting for transfers between devices  12.7 us (12%)
  local copies, waits for them, and re-layouts  10.1 us (9%)
    pallas_call x1, Pallas kernels, ocean(): pl.pallas_call(ocean_kernel, out_shape=(shaped(TILE, TILE), shaped(8, TIL...  19.8 us
    ppermute x13, starting transfers between devices, shifted(): lax.ppermute(value, axis, [(i, (i + step) % count) for i in range(count)])  16.7 us
    all_to_all x1, starting transfers between devices, on_device(): inbound = lax.all_to_all(outbound, ('gx', 'gy'), 0, 0, tiled=True)  12.2 us
    unnamed x45, local copies, waits for them, and re-layouts  10.1 us
    pallas_call x1, Pallas kernels, lookup(): pl.pallas_call(lookup_kernel, out_shape=shaped(steps * per, NF + 1, LN),...  7.59 us
    all_to_all x1, starting transfers between devices, on_device(): landed = lax.all_to_all(lifted, ('gx', 'gy'), 0, 0, tiled=True)  7.4 us
    all_to_all x1, waiting for transfers between devices, on_device(): inbound = lax.all_to_all(outbound, ('gx', 'gy'), 0, 0, tiled=True)  7.15 us
    all_to_all x1, waiting for transfers between devices, on_device(): landed = lax.all_to_all(lifted, ('gx', 'gy'), 0, 0, tiled=True)  5.53 us
  transfers between devices with their start and end apart: 15, of which 2 were waited for; matrix products, arithmetic and copies ran while one was open for 3% of the time, Pallas kernels for 34%

commit v1 on v0

--- a/solution.py
+++ b/solution.py
@@ -25,6 +25,10 @@
     return pl.CostEstimate(flops=int(us * 2e8), bytes_accessed=1 << 20, transcendentals=0)
 
 
+def limit(mib):
+    return pltpu.CompilerParams(vmem_limit_bytes=mib << 20)
+
+
 def shaped(*dims):
     return jax.ShapeDtypeStruct(dims, f32)
 
@@ -57,6 +61,11 @@
     return [jnp.concatenate([jnp.where(h, v, zero) for h in hits], axis=0) for v in value]
 
 
+def joined(left, right):
+    whole = [jnp.concatenate([r[i] for i in range(8)], axis=1) for r in (left, right)]
+    return lax.dot_general(*whole, NT, preferred_element_type=f32)
+
+
 def pick(table, index, which, sources):
     found = jnp.zeros(index.shape, f32)
     for s in range(sources):
@@ -97,53 +106,67 @@
     return after - before
 
 
-def lookup_kernel(meta, weight, cell, height, out, high_low):
-    @pl.when(pl.program_id(0) == 0)
-    def _():
-        high, low = split(height[...])
-        high_low[0:TILE] = high
-        high_low[TILE:] = low
-
+def arrange_kernel(weight, out):
+    for t in range(SLAB // LN):
+        out[t, 0:NF, :] = weight[:, t * LN : (t + 1) * LN]
+        out[t, NF : NF + 1, :] = jnp.zeros((1, LN), f32)
+
+
+def arrange(weight):
+    steps = weight.shape[1] // SLAB
+    per = SLAB // LN
+    return pl.pallas_call(
+        arrange_kernel,
+        out_shape=shaped(steps * per, NF + 1, LN),
+        grid=(steps,),
+        in_specs=[pl.BlockSpec((NF, SLAB), lambda s: (0, s))],
+        out_specs=pl.BlockSpec((per, NF + 1, LN), lambda s: (s, 0, 0)),
+        compiler_params=limit(8),
+        cost_estimate=cost(1),
+        name="arrange",
+    )(weight)
+
+
+def lookup_kernel(meta, cell, height, out, high_low):
+    high, low = split(height[...])
+    high_low[0:TILE] = high
+    high_low[TILE:] = low
     layer = meta[0]
-    base = pl.program_id(0) * SLAB
     one = jnp.ones((16, TILE), bf16)
     ids = lax.broadcasted_iota(jnp.int32, (TILE, TILE), 0)
-    for pair in range(SLAB // TILE):
-        start = pl.multiple_of(base + pair * TILE, TILE)
-        cells = cell[0, 0:1, pl.ds(start, TILE)]
-        for n in range(1, cell.shape[1]):
-            cells = jnp.where(layer == n, cell[0, n : n + 1, pl.ds(start, TILE)], cells)
-        rows, cols = (cells >> 8, cells & 255)
-        (hot,) = one_hot(cols, TILE, [one])
-        both = jnp.dot(high_low[...], hot, preferred_element_type=f32)
-        found = both[:TILE] + both[TILE:]
-        values = jnp.sum(jnp.where(ids == rows, found, 0.0), axis=0, keepdims=True)
-        for half in range(2):
-            t = 2 * pair + half
-            out[t, 0:NF, :] = weight[0, 0, :, t * LN : (t + 1) * LN]
-            out[t, NF : NF + 1, :] = values[:, half * LN : (half + 1) * LN]
-
-
-def lookup(meta, ocean_weight, ocean_cell, height):
-    steps = ocean_cell.shape[2] // SLAB
-    per = SLAB // LN
+
+    def pair(c, carry):
+        for half in range(4):
+            t = c * 8 + half * 2
+            start = pl.multiple_of(t * LN, TILE)
+            cells = cell[0, 0:1, pl.ds(start, TILE)]
+            for n in range(1, cell.shape[1]):
+                cells = jnp.where(layer == n, cell[0, n : n + 1, pl.ds(start, TILE)], cells)
+            rows, cols = (cells >> 8, cells & 255)
+            (hot,) = one_hot(cols, TILE, [one])
+            both = jnp.dot(high_low[...], hot, preferred_element_type=f32)
+            found = both[:TILE] + both[TILE:]
+            values = jnp.sum(jnp.where(ids == rows, found, 0.0), axis=0, keepdims=True)
+            out[pl.ds(t, 1), :] = values[:, 0:LN]
+            out[pl.ds(t + 1, 1), :] = values[:, LN:]
+        return carry
+
+    lax.fori_loop(0, out.shape[0] // 8, pair, 0)
+
+
+def lookup(meta, ocean_cell, height):
+    smem = pl.BlockSpec(memory_space=pltpu.SMEM)
+    vmem = pl.BlockSpec(memory_space=pltpu.VMEM)
     return pl.pallas_call(
         lookup_kernel,
-        out_shape=shaped(steps * per, NF + 1, LN),
-        grid_spec=pltpu.PrefetchScalarGridSpec(
-            num_scalar_prefetch=1,
-            grid=(steps,),
-            in_specs=[
-                pl.BlockSpec((1, 1, NF, SLAB), lambda s, m: (0, m[0], 0, s)),
-                pl.BlockSpec(ocean_cell.shape, lambda s, m: (0, 0, 0)),
-                pl.BlockSpec(height.shape, lambda s, m: (0, 0)),
-            ],
-            out_specs=pl.BlockSpec((per, NF + 1, LN), lambda s, m: (s, 0, 0)),
-            scratch_shapes=[pltpu.VMEM((2 * TILE, TILE), bf16)],
-        ),
-        cost_estimate=cost(4),
+        out_shape=shaped(ocean_cell.shape[2] // LN, LN),
+        in_specs=[smem, vmem, vmem],
+        out_specs=vmem,
+        scratch_shapes=[pltpu.VMEM((2 * TILE, TILE), bf16)],
+        compiler_params=limit(16),
+        cost_estimate=cost(6),
         name="lookup",
-    )(meta, ocean_weight, ocean_cell, height)
+    )(meta, ocean_cell, height)
 
 
 def spread_jacobians(jacobians, spread):
@@ -151,7 +174,7 @@
         for p in range(NQ):
             for q in range(NQ):
                 at = ((d * NQ + p) * NQ + q) * 8
-                spread[at : at + 8] = jnp.broadcast_to(jacobians[d, p, q : q + 1, :], (8, LN))
+                spread[at : at + 8] = jnp.broadcast_to(jacobians[p, q, d : d + 1, :], (8, LN))
 
 
 def couple(spread, dof, coupled):
@@ -185,7 +208,8 @@
 def face_rows(projection, pad):
     pad[...] = jnp.zeros((LN, LN), f32)
     for f in range(4):
-        pad[f * 16 : f * 16 + NF, 0:NB] = projection[f]
+        for a in range(NF):
+            pad[f * 16 + a : f * 16 + a + 1, 0:NB] = projection[a, f : f + 1, :]
     return pad
 
 
@@ -244,77 +268,90 @@
             pltpu.VMEM((LN, LN), f32),
             pltpu.VMEM((8, LN), jnp.int32),
         ],
-        cost_estimate=cost(10),
+        compiler_params=limit(24),
+        cost_estimate=cost(5),
         name="predict",
     )(state, jacobians, stiffness, projection, send, east, north)
 
 
-def uplift_kernel(inbound, trace, floor, out):
+def uplift_kernel(inbound, trace, floor, heights, out):
     def tile(r, carry):
         face = jnp.broadcast_to(floor[pl.ds(r, 1), :], (16, LN))
         found = pick(
             lambda s: trace[s * 16 : (s + 1) * 16, 8 * LN : 9 * LN], face & 127, face >> 7, 4
         )
-        out[pl.ds(r, 1), :] = jnp.sum(inbound[r] * found, axis=0, keepdims=True)
+        out[r, 0:1, :] = jnp.sum(inbound[r] * found, axis=0, keepdims=True)
+        out[r, 1:2, :] = heights[pl.ds(r, 1), :]
         return carry
 
     lax.fori_loop(0, floor.shape[0], tile, 0, unroll=8)
 
 
-def uplift(inbound, trace, floor):
-    return pl.pallas_call(
-        uplift_kernel, out_shape=shaped(*floor.shape), cost_estimate=cost(2), name="uplift"
-    )(inbound, trace, floor)
-
-
-def volume_kernel(
-    state, jacobians, stiffness, integral, inbound, floor, base, load, spread, coupled, pad, left, right
-):
+def uplift(inbound, trace, floor, heights):
+    return pl.pallas_call(
+        uplift_kernel,
+        out_shape=shaped(floor.shape[0], 2, LN),
+        compiler_params=limit(16),
+        cost_estimate=cost(2),
+        name="uplift",
+    )(inbound, trace, floor, heights)
+
+
+def volume_kernel(state, jacobians, stiffness, integral, base, spread, coupled, pad):
     spread_jacobians(jacobians, spread)
     coupled[...] = jnp.zeros((LN, EL), f32)
     couple(spread, integral, coupled)
     volume = dot3(stiffness_rows(stiffness, pad, True), coupled[...])
     base[...] = volume
     for q in range(NQ):
-        here = pl.ds(q * LN, LN)
-        base[0:NB, here] = volume[0:NB, q * LN : (q + 1) * LN] + state[q]
-    zero = jnp.zeros((16, LN), bf16)
-    one = jnp.ones((16, LN), bf16)
-
-    def chunk(c, total):
-        for i in range(8):
-            r = c * 8 + i
-            lanes = slice(i * LN, (i + 1) * LN)
-            face = floor[pl.ds(r, 1), :]
-            part = inbound[r]
-            high, low = split(part * part[NF : NF + 1, :])
-            (hot,) = one_hot(face & 127, LN, [one])
-            right[:, lanes] = hot
-            side = jnp.broadcast_to((face >> 7).astype(f32), (16, LN)).astype(bf16)
-            for f in range(4):
-                hit = side == jnp.full((16, LN), f, bf16)
-                left[f * 16 : (f + 1) * 16, lanes] = jnp.where(hit, high, zero)
-                left[64 + f * 16 : 64 + (f + 1) * 16, lanes] = jnp.where(hit, low, zero)
-        return total + lax.dot_general(left[...], right[...], NT, preferred_element_type=f32)
-
-    total = lax.fori_loop(0, floor.shape[0] // 8, chunk, jnp.zeros((LN, LN), f32))
-    load[...] = total[:64] + total[64:]
-
-
-def volume(state, jacobians, stiffness, integral, inbound, floor):
+        base[0:NB, q * LN : (q + 1) * LN] = volume[0:NB, q * LN : (q + 1) * LN] + state[q]
+
+
+def volume(state, jacobians, stiffness, integral):
     return pl.pallas_call(
         volume_kernel,
-        out_shape=(shaped(40, EL), shaped(64, LN)),
+        out_shape=shaped(40, EL),
         scratch_shapes=[
             pltpu.VMEM((243 * 8, LN), f32),
             pltpu.VMEM((LN, EL), f32),
             pltpu.VMEM((LN, LN), f32),
-            pltpu.VMEM((LN, SLAB), bf16),
-            pltpu.VMEM((LN, SLAB), bf16),
         ],
-        cost_estimate=cost(6),
+        compiler_params=limit(16),
+        cost_estimate=cost(3),
         name="volume",
-    )(state, jacobians, stiffness, integral, inbound, floor)
+    )(state, jacobians, stiffness, integral)
+
+
+def pressure_kernel(inbound, landed, floor, load, left, right):
+    zero = jnp.zeros((16, LN), bf16)
+    one = jnp.ones((16, LN), bf16)
+
+    def chunk(c, total):
+        for i in range(8):
+            r = c * 8 + i
+            face = floor[pl.ds(r, 1), :]
+            high, low = split(inbound[r] * landed[r, 1:2, :])
+            (right[i],) = one_hot(face & 127, LN, [one])
+            side = jnp.broadcast_to((face >> 7).astype(f32), (16, LN)).astype(bf16)
+            for f in range(4):
+                hit = side == jnp.full((16, LN), f, bf16)
+                left[i, f * 16 : (f + 1) * 16] = jnp.where(hit, high, zero)
+                left[i, 64 + f * 16 : 64 + (f + 1) * 16] = jnp.where(hit, low, zero)
+        return total + joined(left, right)
+
+    total = lax.fori_loop(0, floor.shape[0] // 8, chunk, jnp.zeros((LN, LN), f32))
+    load[...] = total[:64] + total[64:]
+
+
+def pressure(inbound, landed, floor):
+    return pl.pallas_call(
+        pressure_kernel,
+        out_shape=shaped(64, LN),
+        scratch_shapes=[pltpu.VMEM((8, LN, LN), bf16), pltpu.VMEM((8, LN, LN), bf16)],
+        compiler_params=limit(16),
+        cost_estimate=cost(3),
+        name="pressure",
+    )(inbound, landed, floor)
 
 
 def flux_kernel(
@@ -338,9 +375,9 @@
             found = jnp.where(hit, side[:, here], found)
         received[:, here] = found
 
-    def face(f, carry):
-        which = jnp.broadcast_to(source[pl.ds(f, 1), :], (16, LN))
-        rows = pl.ds(pl.multiple_of(f * 16, 16), 16)
+    for f in range(4):
+        which = jnp.broadcast_to(source[f : f + 1, :], (16, LN))
+        rows = slice(f * 16, (f + 1) * 16)
         total = [None] * NQ
         for q in range(NQ):
             here = slice(q * LN, (q + 1) * LN)
@@ -350,13 +387,10 @@
                 which & 127, which >> 7, 5,
             )
             for p in range(NQ):
-                term = mine * own[f, q, p : p + 1, :] + remote * other[f, q, p : p + 1, :]
+                term = mine * own[q, p, f : f + 1, :] + remote * other[q, p, f : f + 1, :]
                 total[p] = term if total[p] is None else total[p] + term
         for p in range(NQ):
             numeric[rows, p * LN : (p + 1) * LN] = total[p]
-        return carry
-
-    lax.fori_loop(0, 4, face, 0)
     numeric[:, 2 * LN : 3 * LN] = numeric[:, 2 * LN : 3 * LN] + load[...]
     taken = dot3(matrix, numeric[...])
     updated = base[...] - taken
@@ -378,14 +412,16 @@
             pltpu.VMEM((16, EL), f32),
             pltpu.VMEM((LN, LN), f32),
         ],
-        cost_estimate=cost(6),
+        compiler_params=limit(16),
+        cost_estimate=cost(4),
         name="flux",
     )(meta, state, base, load, trace, *received, source, own, other, projection, mask)
 
 
 def ocean_kernel(
     meta, first, second, third, fourth, cell, below_x, above_x, below_y, above_y,
-    height, east, north, depth, new_height, edges, left, right, total, lifts,
+    height, east, north, depth, new_height, edges,
+    left_a, right_a, left_b, right_b, total, lifts,
 ):
     layers = meta[3]
     per = first.shape[0]
@@ -393,26 +429,29 @@
     one = jnp.ones((16, LN), bf16)
     for shift, values in enumerate((first, second, third, fourth)):
         layer = lax.rem(meta[0] - shift + layers, layers)
-        lifts[pl.ds(pl.multiple_of(layer * per, 8), per)] = values[...]
-    for layer in range(4):
-
-        def chunk(c, carry):
-            for i in range(8):
-                r = c * 8 + i
-                lanes = slice(i * LN, (i + 1) * LN)
-                start = pl.multiple_of(r * LN, LN)
-                cells = cell[0, layer : layer + 1, pl.ds(start, LN)]
-                value = jnp.broadcast_to(lifts[pl.ds(layer * per + r, 1), :], (16, LN))
-                high, low = one_hot(cells >> 8, TILE, split(value))
-                left[0:TILE, lanes] = high
-                left[TILE:, lanes] = low
-                (right[:, lanes],) = one_hot(cells & 255, TILE, [one])
-            total[...] += lax.dot_general(
-                left[...], right[...], NT, preferred_element_type=f32
-            )
-            return carry
-
-        lax.fori_loop(0, per // 8, chunk, 0)
+        lifts[pl.ds(pl.multiple_of(layer * per, 8), per)] = values[:, 0, :]
+
+    def build(c, left, right):
+        for half in range(2):
+            t = c * 2 + half
+            cells = cell[0, :, pl.ds(pl.multiple_of(t * LN, LN), LN)]
+            for layer in range(4):
+                here = cells[layer : layer + 1, :]
+                value = jnp.broadcast_to(lifts[pl.ds(layer * per + t, 1), :], (16, LN))
+                high, low = one_hot(here >> 8, TILE, split(value))
+                left[half * 4 + layer, 0:TILE] = high
+                left[half * 4 + layer, TILE:] = low
+                (right[half * 4 + layer],) = one_hot(here & 255, TILE, [one])
+
+    def chunks(c, carry):
+        build(2 * c + 1, left_b, right_b)
+        total[...] += joined(left_a, right_a)
+        build(jnp.minimum(2 * c + 2, per // 2 - 1), left_a, right_a)
+        total[...] += joined(left_b, right_b)
+        return carry
+
+    build(0, left_a, right_a)
+    lax.fori_loop(0, per // 4, chunks, 0)
     source = total[0:TILE] + total[TILE:]
     rim = slice(EL, EDGE)
     low_x = jnp.where(meta[1] > 0, below_x[1:2, rim], 0.0)
@@ -439,11 +478,14 @@
         in_specs=[smem] + [vmem] * 13,
         out_specs=(vmem, vmem),
         scratch_shapes=[
-            pltpu.VMEM((2 * TILE, SLAB), bf16),
-            pltpu.VMEM((TILE, SLAB), bf16),
+            pltpu.VMEM((8, 2 * TILE, LN), bf16),
+            pltpu.VMEM((8, TILE, LN), bf16),
+            pltpu.VMEM((8, 2 * TILE, LN), bf16),
+            pltpu.VMEM((8, TILE, LN), bf16),
             pltpu.VMEM((2 * TILE, TILE), f32),
             pltpu.VMEM((4 * layers[0].shape[0], LN), f32),
         ],
+        compiler_params=limit(32),
         cost_estimate=cost(10),
         name="ocean",
     )(meta, *layers, cell, *received[:4], height, east, north, depth)
@@ -467,6 +509,7 @@
         out_shape=(shaped(TILE, TILE), shaped(TILE, TILE)),
         in_specs=[smem] + [vmem] * 7,
         out_specs=(vmem, vmem),
+        compiler_params=limit(16),
         cost_estimate=cost(2),
         name="flow",
     )(meta, height, east, north, *received)
@@ -503,16 +546,22 @@
         meta = jnp.where(spot == n + 3, lax.axis_size(axis), meta)
     floor = seafloor_face.reshape(-1, LN)
     mask = cluster_mask.reshape(1, LN)
-    outbound = lookup(meta, ocean_weight, ocean_cell, height)
-    inbound = lax.all_to_all(outbound, ("gx", "gy"), 0, 0, tiled=True)
+    jacobians, flux_self, flux_other = (
+        jnp.transpose(x, (1, 2, 0, 3)) for x in (jacobians, flux_self, flux_other)
+    )
+    projection = jnp.transpose(projection, (1, 0, 2))
+    weight = lax.dynamic_index_in_dim(ocean_weight[0], lax.axis_index("gz"), 0, keepdims=False)
+    inbound = lax.all_to_all(arrange(weight), ("gx", "gy"), 0, 0, tiled=True)
     integral, trace, sent = predict(
         element_state, jacobians, stiffness, projection, send_faces, east_flow, north_flow
     )
-    lifted = uplift(inbound, trace, floor)
+    heights = lookup(meta, ocean_cell, height)
+    lifted = uplift(inbound, trace, floor, heights)
     landed = lax.all_to_all(lifted, ("gx", "gy"), 0, 0, tiled=True)
     received = [shifted(sent, axis, step) for axis in ("gx", "gy", "gz") for step in (1, -1)]
     layers = [landed] + [shifted(landed, "gz", step) for step in (1, 2, 3)]
-    base, load = volume(element_state, jacobians, stiffness, integral, inbound, floor)
+    base = volume(element_state, jacobians, stiffness, integral)
+    load = pressure(inbound, landed, floor)
     new_height, edges = ocean(
         meta, layers, ocean_cell, received, height, east_flow, north_flow, water_depth
     )

time: 109 us -> 90.4 us (0.83)
  Pallas kernels: 46.4 us -> 34.6 us
  waiting for transfers between devices: 12.7 us -> 7.49 us
    pallas_call x1, Pallas kernels: 19.8 us -> 15.1 us  [ocean(): pl.pallas_call(ocean_kernel, out_shape=(shaped(TILE, TILE), shaped(8, TIL...]
    pallas_call x3 -> x5, Pallas kernels: 16.1 us -> 12.3 us  [the longest x1 4.24 us: lookup(): pl.pallas_call(lookup_kernel, out_shape=shaped(ocean_cell.shape[2] // LN,...]
    all_to_all x1, waiting for transfers between devices: 5.53 us -> 2.35 us  [on_device(): landed = lax.all_to_all(lifted, ('gx', 'gy'), 0, 0, tiled=True)]
    all_to_all x1, waiting for transfers between devices: 7.15 us -> 5.1 us  [on_device(): inbound = lax.all_to_all(arrange(weight), ('gx', 'gy'), 0, 0, tiled=True)]
    pallas_call x1, Pallas kernels: 5.02 us -> 2.99 us  [predict(): pl.pallas_call(predict_kernel, out_shape=(shaped(40, EL), shaped(64, EL),...]
    unnamed x45 -> x59, local copies, waits for them, and re-layouts: 10.1 us -> 9.27 us
  transfers between devices with their start and end apart: 15 -> 15, of which waited for: 2 -> 2; matrix products, arithmetic and copies ran while one was open for 3% -> 0% of each run, Pallas kernels for 34% -> 32%
where the time goes in v1:
time: 90.4 us; the launch traced here: 88.9 us
  starting transfers between devices  36 us (40%)
  Pallas kernels  34.6 us (38%)
  local copies, waits for them, and re-layouts  9.82 us (11%)
  waiting for transfers between devices  7.49 us (8%)
  between operations  1 us (1%)
    ppermute x13, starting transfers between devices, shifted(): lax.ppermute(value, axis, [(i, (i + step) % count) for i in range(count)])  16.6 us
    pallas_call x1, Pallas kernels, ocean(): pl.pallas_call(ocean_kernel, out_shape=(shaped(TILE, TILE), shaped(8, TIL...  15.1 us
    all_to_all x1, starting transfers between devices, on_device(): inbound = lax.all_to_all(arrange(weight), ('gx', 'gy'), 0, 0, tiled=True)  12.2 us
    unnamed x59, local copies, waits for them, and re-layouts  9.27 us
    all_to_all x1, starting transfers between devices, on_device(): landed = lax.all_to_all(lifted, ('gx', 'gy'), 0, 0, tiled=True)  7.18 us
    all_to_all x1, waiting for transfers between devices, on_device(): inbound = lax.all_to_all(arrange(weight), ('gx', 'gy'), 0, 0, tiled=True)  5.1 us
    pallas_call x1, Pallas kernels, lookup(): pl.pallas_call(lookup_kernel, out_shape=shaped(ocean_cell.shape[2] // LN,...  4.24 us
    pallas_call x1, Pallas kernels, predict(): pl.pallas_call(predict_kernel, out_shape=(shaped(40, EL), shaped(64, EL),...  2.99 us
  transfers between devices with their start and end apart: 15, of which 2 were waited for; matrix products, arithmetic and copies ran while one was open for 0% of the time, Pallas kernels for 32%

profile of v1, /device:TPU:7, one launch (start us, length us, event | category | flops | bytes accessed | tf_op | source)
XLA Modules:
  0.0 88.9 jit_solution(14625949256190010144)
XLA Ops:
  0.7 1.5 %copy-done = f32[1,4,15,8192]{3,1,2,0:T(4,128)S(1)} copy-done((f32[1,4,15,8192]{3,1,2,0:T(4,128)S(1)}, f32[1,4,15,8192]{3,1,2,0:T(4,128)}, u32[]{:S(2)}) %copy-start) | copy-done | bytes 1966104
  3.1 2.6 %arrange.1 = f32[64,16,128]{2,1,0:T(8,128)} custom-call(f32[15,8192]{1,0:T(8,128)S(1)} %bitcast.9), custom_call_target="tpu_custom_call" | custom-call | flops 200000000 | bytes 1048576 | tf_op jit(solution)/shard_map/arrange/pallas_call | solution.py:118
  5.7 12.2 %all-to-all-start = ((f32[64,16,128]{2,1,0:T(8,128)}), f32[64,16,128]{2,1,0:T(8,128)S(1)}, u32[]{:S(2)}, u32[]{:S(2)}) async-start(f32[64,16,128]{2,1,0:T(8,128)} %arrange.1), calls=%async_computation | async-start | bytes 1048576 | tf_op jit(solution)/shard_map/all_to_all | solution.py:554
  18.0 0.9 %copy-done.6 = f32[3,9,9,128]{3,0,2,1:T(4,128)S(1)} copy-done((f32[3,9,9,128]{3,0,2,1:T(4,128)S(1)}, f32[3,9,9,128]{3,0,2,1:T(4,128)}, u32[]{:S(2)}) %copy-start.6) | copy-done | bytes 124440
  19.7 3.0 %predict.1 = (f32[40,1152]{1,0:T(8,128)S(1)}, f32[64,1152]{1,0:T(8,128)S(1)}, f32[16,1408]{1,0:T(8,128)S(1)}) custom-call(f32[9,35,128]{2,1,0:T(8,128)S(1)} %copy-done.5, f32[9,9,3,128]{3,2,1,0:T(4,128)S(1)} %bitcast.10, f32[3,35,35]{2,1,0:T(8,128)S(1)} %copy-done.14, f32[15,4,35]{2,1,0:T(4,128)S(1)} %bitcast.16, s32[6,16]{1,0:T(8,128)S(1)} %copy-done.20, ...), custom_call_target="tpu_custom_call" | custom-call | flops 1000000000 | bytes 1048576 | tf_op jit(solution)/shard_map/predict/pallas_call | solution.py:261
  24.8 4.2 %lookup.1.heights = f32[64,128]{1,0:T(8,128)S(1)} custom-call(s32[8]{0:T(128)S(1)} %compare_select_fusion.5.meta, s32[1,4,8192]{2,1,0:T(4,128)S(1)} %copy-done.10, f32[256,256]{1,0:T(8,128)S(1)} %copy-done.1), custom_call_target="tpu_custom_call" | custom-call | flops 1200000000 | bytes 1048576 | tf_op jit(solution)/shard_map/lookup/pallas_call | solution.py:160
  29.0 5.1 %all-to-all-done.inbound = f32[64,16,128]{2,1,0:T(8,128)S(1)} async-done(((f32[64,16,128]{2,1,0:T(8,128)}), f32[64,16,128]{2,1,0:T(8,128)S(1)}, u32[]{:S(2)}, u32[]{:S(2)}) %all-to-all-start) | async-done | bytes 524320 | tf_op jit(solution)/shard_map/all_to_all | solution.py:554
  34.1 1.0 %copy-done.25 = f32[64,1152]{1,0:T(8,128)S(1)} copy-done((f32[64,1152]{1,0:T(8,128)S(1)}, f32[64,1152]{1,0:T(8,128)}, u32[]{:S(2)}) %copy-start.25) | copy-done | bytes 294936
  35.1 2.2 %uplift.1 = f32[64,2,128]{2,1,0:T(2,128)} custom-call(f32[64,16,128]{2,1,0:T(8,128)S(1)} %all-to-all-done.inbound, f32[64,1152]{1,0:T(8,128)S(1)} %copy-done.25, s32[64,128]{1,0:T(8,128)S(1)} %bitcast.14, f32[64,128]{1,0:T(8,128)S(1)} %lookup.1.heights), custom_call_target="tpu_custom_call" | custom-call | flops 400000000 | bytes 1048576 | tf_op jit(solution)/shard_map/uplift/pallas_call | solution.py:291
  37.3 7.2 %all-to-all-start.1 = ((f32[64,2,128]{2,1,0:T(2,128)}), f32[64,2,128]{2,1,0:T(2,128)S(1)}, u32[]{:S(2)}, u32[]{:S(2)}) async-start(f32[64,2,128]{2,1,0:T(2,128)} %uplift.1), calls=%async_computation.1 | async-start | bytes 131072 | tf_op jit(solution)/shard_map/all_to_all | solution.py:560
  44.9 2.6 %collective-permute-start.2 = (f32[16,1408]{1,0:T(8,128)}, f32[16,1408]{1,0:T(8,128)}, u32[]{:S(2)}, u32[]{:S(2)}) collective-permute-start(f32[16,1408]{1,0:T(8,128)} %copy-done.12), channel_id=1, source_target_pairs={{0,4},{4,8},{8,12},{12,16},{16,20},{20,24},{24,28},{28,0},{1,5},{5... | collective-permute-start | bytes 270344 | tf_op jit(solution)/shard_map/ppermute | solution.py:520
  47.4 2.7 %collective-permute-start.1 = (f32[16,1408]{1,0:T(8,128)}, f32[16,1408]{1,0:T(8,128)}, u32[]{:S(2)}, u32[]{:S(2)}) collective-permute-start(f32[16,1408]{1,0:T(8,128)} %copy-done.12), channel_id=1, source_target_pairs={{0,224},{32,0},{64,32},{96,64},{128,96},{160,128},{192,160},{224,1... | collective-permute-start | bytes 270344 | tf_op jit(solution)/shard_map/ppermute | solution.py:520
  50.1 2.4 %all-to-all-done.1.landed.first = f32[64,2,128]{2,1,0:T(2,128)S(1)} async-done(((f32[64,2,128]{2,1,0:T(2,128)}), f32[64,2,128]{2,1,0:T(2,128)S(1)}, u32[]{:S(2)}, u32[]{:S(2)}) %all-to-all-start.1) | async-done | bytes 65568 | tf_op jit(solution)/shard_map/all_to_all | solution.py:560
  52.5 2.7 %collective-permute-start.8 = (f32[64,2,128]{2,1,0:T(2,128)S(1)}, f32[64,2,128]{2,1,0:T(2,128)S(1)}, u32[]{:S(2)}, u32[]{:S(2)}) collective-permute-start(f32[64,2,128]{2,1,0:T(2,128)S(1)} %all-to-all-done.1.landed.first), channel_id=1, source_target_pairs={{0,3},{1,0},{2,1},{3,2},{4,7},{5,4},{6,5},{7,6},{8,11},{9,8},{10,9... | collective-permute-start | bytes 196616 | tf_op jit(solution)/shard_map/ppermute | solution.py:520
  56.3 0.9 %copy-done.7 = f32[3,9,9,128]{3,0,2,1:T(4,128)S(1)} copy-done((f32[3,9,9,128]{3,0,2,1:T(4,128)S(1)}, f32[3,9,9,128]{3,0,2,1:T(4,128)}, u32[]{:S(2)}) %copy-start.7) | copy-done | bytes 124440
  58.0 0.9 %copy-done.28 = f32[40,1152]{1,0:T(8,128)S(1)} copy-done((f32[40,1152]{1,0:T(8,128)S(1)}, f32[40,1152]{1,0:T(8,128)}, u32[]{:S(2)}) %copy-start.28) | copy-done | bytes 184344
  59.8 2.3 %pressure.1.load = f32[64,128]{1,0:T(8,128)S(1)} custom-call(f32[64,16,128]{2,1,0:T(8,128)S(1)} %all-to-all-done.inbound, f32[64,2,128]{2,1,0:T(2,128)S(1)} %all-to-all-done.1.landed.first, s32[64,128]{1,0:T(8,128)S(1)} %bitcast.15), custom_call_target="tpu_custom_call" | custom-call | flops 600000000 | bytes 1048576 | tf_op jit(solution)/shard_map/pressure/pallas_call | solution.py:347
  62.3 2.1 %collective-permute-start.5 = (f32[16,1408]{1,0:T(8,128)S(1)}, f32[16,1408]{1,0:T(8,128)S(1)}, u32[]{:S(2)}, u32[]{:S(2)}) collective-permute-start(f32[16,1408]{1,0:T(8,128)S(1)} %copy-done.13), channel_id=1, source_target_pairs={{0,3},{1,0},{2,1},{3,2},{4,7},{5,4},{6,5},{7,6},{8,11},{9,8},{10,9... | collective-permute-start | bytes 270344 | tf_op jit(solution)/shard_map/ppermute | solution.py:520
  64.4 15.1 %ocean.1 = (f32[256,256]{1,0:T(8,128)}, f32[8,256]{1,0:T(8,128)S(1)}) custom-call(s32[8]{0:T(128)S(1)} %compare_select_fusion.5.meta, f32[64,2,128]{2,1,0:T(2,128)S(1)} %all-to-all-done.1.landed.first, f32[64,2,128]{2,1,0:T(2,128)S(1)} %collective-permute-done.6.second, f32[64,2,128]{2,1,0:T(2,128)S(1)} %collective-permute-done.7.third, ...), custom_call_target="tpu_custom_call" | custom-call | flops 2000000000 | bytes 1048576 | tf_op jit(solution)/shard_map/ocean/pallas_call | solution.py:475
  79.6 1.5 %collective-permute-start.12 = (f32[8,256]{1,0:T(8,128)S(1)}, f32[8,256]{1,0:T(8,128)S(1)}, u32[]{:S(2)}, u32[]{:S(2)}) collective-permute-start(f32[8,256]{1,0:T(8,128)S(1)} %get-tuple-element.15), channel_id=1, source_target_pairs={{0,28},{4,0},{8,4},{12,8},{16,12},{20,16},{24,20},{28,24},{1,29},{... | collective-permute-start | bytes 24584 | tf_op jit(solution)/shard_map/ppermute | solution.py:520
  81.1 2.1 %collective-permute-start.11 = (f32[8,256]{1,0:T(8,128)S(1)}, f32[8,256]{1,0:T(8,128)S(1)}, u32[]{:S(2)}, u32[]{:S(2)}) collective-permute-start(f32[8,256]{1,0:T(8,128)S(1)} %get-tuple-element.15), channel_id=1, source_target_pairs={{0,4},{4,8},{8,12},{12,16},{16,20},{20,24},{24,28},{28,0},{1,5},{5... | collective-permute-start | bytes 24584 | tf_op jit(solution)/shard_map/ppermute | solution.py:520
  83.3 1.3 %collective-permute-start.9 = (f32[8,256]{1,0:T(8,128)S(1)}, f32[8,256]{1,0:T(8,128)S(1)}, u32[]{:S(2)}, u32[]{:S(2)}) collective-permute-start(f32[8,256]{1,0:T(8,128)S(1)} %get-tuple-element.15), channel_id=1, source_target_pairs={{0,32},{32,64},{64,96},{96,128},{128,160},{160,192},{192,224},{224... | collective-permute-start | bytes 24584 | tf_op jit(solution)/shard_map/ppermute | solution.py:520
  84.7 2.7 %flux.1 = f32[9,35,128]{2,1,0:T(8,128)} custom-call(s32[8]{0:T(128)S(1)} %compare_select_fusion.5.meta, f32[9,35,128]{2,1,0:T(8,128)S(1)} %copy-done.5, f32[40,1152]{1,0:T(8,128)S(1)} %volume.1.base, f32[64,128]{1,0:T(8,128)S(1)} %pressure.1.load, f32[64,1152]{1,0:T(8,128)S(1)} %copy-done.26, f32[16,1408]{1,0:T(8,128)} %collective-permute-done.below_x, ...), custom_call_target="tpu_custom_call" | custom-call | flops 800000000 | bytes 1048576 | tf_op jit(solution)/shard_map/flux/pallas_call | solution.py:405
  87.3 1.6 %flow.1 = (f32[256,256]{1,0:T(8,128)}, f32[256,256]{1,0:T(8,128)}) custom-call(s32[8]{0:T(128)S(1)} %compare_select_fusion.5.meta, f32[256,256]{1,0:T(8,128)S(1)} %copy-done.23, f32[256,256]{1,0:T(8,128)S(1)} %copy-done.3, f32[256,256]{1,0:T(8,128)S(1)} %copy-done.4, f32[8,256]{1,0:T(8,128)S(1)} %collective-permute-done.9.below_x, ...), custom_call_target="tpu_custom_call" | custom-call | flops 400000000 | bytes 1048576 | tf_op jit(solution)/shard_map/flow/pallas_call | solution.py:507
  (76 shorter events, 7.0 us)
Async XLA Ops:
  2.2 15.8 %copy-start.5 = (f32[9,35,128]{2,1,0:T(8,128)S(1)}, f32[9,35,128]{2,1,0:T(8,128)}, u32[]{:S(2)}) copy-start(f32[9,35,128]{2,1,0:T(8,128)} %state.5) | copy-start | bytes 483844
  2.2 15.8 %copy-start.14 = (f32[3,35,35]{2,1,0:T(8,128)S(1)}, f32[3,35,35]{2,1,0:T(8,128)}, u32[]{:S(2)}) copy-start(f32[3,35,35]{2,1,0:T(8,128)} %stiffness.3) | copy-start | bytes 44104
  2.2 15.8 %copy-start.20 = (s32[6,16]{1,0:T(8,128)S(1)}, s32[6,16]{1,0:T(8,128)}, u32[]{:S(2)}) copy-start(s32[6,16]{1,0:T(8,128)} %send.1) | copy-start | bytes 1156
  5.7 28.4 %all-to-all-start = ((f32[64,16,128]{2,1,0:T(8,128)}), f32[64,16,128]{2,1,0:T(8,128)S(1)}, u32[]{:S(2)}, u32[]{:S(2)}) async-start(f32[64,16,128]{2,1,0:T(8,128)} %arrange.1), calls=%async_computation | async-start | bytes 1048576 | tf_op jit(solution)/shard_map/all_to_all | solution.py:554
  37.3 15.2 %all-to-all-start.1 = ((f32[64,2,128]{2,1,0:T(2,128)}), f32[64,2,128]{2,1,0:T(2,128)S(1)}, u32[]{:S(2)}, u32[]{:S(2)}) async-start(f32[64,2,128]{2,1,0:T(2,128)} %uplift.1), calls=%async_computation.1 | async-start | bytes 131072 | tf_op jit(solution)/shard_map/all_to_all | solution.py:560
  44.5 10.8 %collective-permute-start.3 = (f32[16,1408]{1,0:T(8,128)}, f32[16,1408]{1,0:T(8,128)}, u32[]{:S(2)}, u32[]{:S(2)}) collective-permute-start(f32[16,1408]{1,0:T(8,128)} %copy-done.12), channel_id=1, source_target_pairs={{0,28},{4,0},{8,4},{12,8},{16,12},{20,16},{24,20},{28,24},{1,29},{... | collective-permute-start | bytes 270344 | tf_op jit(solution)/shard_map/ppermute | solution.py:520
  44.9 10.7 %collective-permute-start.2 = (f32[16,1408]{1,0:T(8,128)}, f32[16,1408]{1,0:T(8,128)}, u32[]{:S(2)}, u32[]{:S(2)}) collective-permute-start(f32[16,1408]{1,0:T(8,128)} %copy-done.12), channel_id=1, source_target_pairs={{0,4},{4,8},{8,12},{12,16},{16,20},{20,24},{24,28},{28,0},{1,5},{5... | collective-permute-start | bytes 270344 | tf_op jit(solution)/shard_map/ppermute | solution.py:520
  47.4 14.8 %collective-permute-start.1 = (f32[16,1408]{1,0:T(8,128)}, f32[16,1408]{1,0:T(8,128)}, u32[]{:S(2)}, u32[]{:S(2)}) collective-permute-start(f32[16,1408]{1,0:T(8,128)} %copy-done.12), channel_id=1, source_target_pairs={{0,224},{32,0},{64,32},{96,64},{128,96},{160,128},{192,160},{224,1... | collective-permute-start | bytes 270344 | tf_op jit(solution)/shard_map/ppermute | solution.py:520
  50.1 14.2 %collective-permute-start = (f32[16,1408]{1,0:T(8,128)}, f32[16,1408]{1,0:T(8,128)}, u32[]{:S(2)}, u32[]{:S(2)}) collective-permute-start(f32[16,1408]{1,0:T(8,128)} %copy-done.12), channel_id=1, source_target_pairs={{0,32},{32,64},{64,96},{96,128},{128,160},{160,192},{192,224},{224... | collective-permute-start | bytes 270344 | tf_op jit(solution)/shard_map/ppermute | solution.py:520
  52.5 11.9 %collective-permute-start.8 = (f32[64,2,128]{2,1,0:T(2,128)S(1)}, f32[64,2,128]{2,1,0:T(2,128)S(1)}, u32[]{:S(2)}, u32[]{:S(2)}) collective-permute-start(f32[64,2,128]{2,1,0:T(2,128)S(1)} %all-to-all-done.1.landed.first), channel_id=1, source_target_pairs={{0,3},{1,0},{2,1},{3,2},{4,7},{5,4},{6,5},{7,6},{8,11},{9,8},{10,9... | collective-permute-start | bytes 196616 | tf_op jit(solution)/shard_map/ppermute | solution.py:520
  55.2 9.1 %collective-permute-start.7 = (f32[64,2,128]{2,1,0:T(2,128)S(1)}, f32[64,2,128]{2,1,0:T(2,128)S(1)}, u32[]{:S(2)}, u32[]{:S(2)}) collective-permute-start(f32[64,2,128]{2,1,0:T(2,128)S(1)} %all-to-all-done.1.landed.first), channel_id=1, source_target_pairs={{0,2},{1,3},{2,0},{3,1},{4,6},{5,7},{6,4},{7,5},{8,10},{9,11},{10,... | collective-permute-start | bytes 196616 | tf_op jit(solution)/shard_map/ppermute | solution.py:520
  55.6 8.8 %collective-permute-start.6 = (f32[64,2,128]{2,1,0:T(2,128)S(1)}, f32[64,2,128]{2,1,0:T(2,128)S(1)}, u32[]{:S(2)}, u32[]{:S(2)}) collective-permute-start(f32[64,2,128]{2,1,0:T(2,128)S(1)} %all-to-all-done.1.landed.first), channel_id=1, source_target_pairs={{0,1},{1,2},{2,3},{3,0},{4,5},{5,6},{6,7},{7,4},{8,9},{9,10},{10,1... | collective-permute-start | bytes 196616 | tf_op jit(solution)/shard_map/ppermute | solution.py:520
  62.2 22.4 %copy-start.8 = (f32[4,9,9,128]{3,0,2,1:T(4,128)S(1)}, f32[4,9,9,128]{3,0,2,1:T(4,128)}, u32[]{:S(2)}) copy-start(f32[4,9,9,128]{3,0,2,1:T(4,128)} %param.20) | copy-start | bytes 497668
  62.2 22.4 %copy-start.9 = (f32[4,9,9,128]{3,0,2,1:T(4,128)S(1)}, f32[4,9,9,128]{3,0,2,1:T(4,128)}, u32[]{:S(2)}) copy-start(f32[4,9,9,128]{3,0,2,1:T(4,128)} %param.21) | copy-start | bytes 497668
  62.2 22.4 %copy-start.19 = (f32[4,15,35]{2,0,1:T(4,128)S(1)}, f32[4,15,35]{2,0,1:T(4,128)}, u32[]{:S(2)}) copy-start(f32[4,15,35]{2,0,1:T(4,128)} %param.19) | copy-start | bytes 25204
  62.2 22.4 %copy-start.21 = (s32[4,128]{1,0:T(4,128)S(1)}, s32[4,128]{1,0:T(4,128)}, u32[]{:S(2)}) copy-start(s32[4,128]{1,0:T(4,128)} %source.1) | copy-start | bytes 6148
  62.2 22.4 %copy-start.22 = (s32[128]{0:T(128)S(1)}, s32[128]{0:T(128)}, u32[]{:S(2)}) copy-start(s32[128]{0:T(128)} %param.24) | copy-start | bytes 1540
  62.3 22.4 %copy-start.26 = (f32[64,1152]{1,0:T(8,128)S(1)}, f32[64,1152]{1,0:T(8,128)}, u32[]{:S(2)}) copy-start(f32[64,1152]{1,0:T(8,128)} %copy-done.24) | copy-start | bytes 884740
  62.3 21.0 %collective-permute-start.5 = (f32[16,1408]{1,0:T(8,128)S(1)}, f32[16,1408]{1,0:T(8,128)S(1)}, u32[]{:S(2)}, u32[]{:S(2)}) collective-permute-start(f32[16,1408]{1,0:T(8,128)S(1)} %copy-done.13), channel_id=1, source_target_pairs={{0,3},{1,0},{2,1},{3,2},{4,7},{5,4},{6,5},{7,6},{8,11},{9,8},{10,9... | collective-permute-start | bytes 270344 | tf_op jit(solution)/shard_map/ppermute | solution.py:520
  64.4 20.2 %collective-permute-start.4 = (f32[16,1408]{1,0:T(8,128)S(1)}, f32[16,1408]{1,0:T(8,128)S(1)}, u32[]{:S(2)}, u32[]{:S(2)}) collective-permute-start(f32[16,1408]{1,0:T(8,128)S(1)} %copy-done.13), channel_id=1, source_target_pairs={{0,1},{1,2},{2,3},{3,0},{4,5},{5,6},{6,7},{7,4},{8,9},{9,10},{10,1... | collective-permute-start | bytes 270344 | tf_op jit(solution)/shard_map/ppermute | solution.py:520
  79.6 7.8 %collective-permute-start.12 = (f32[8,256]{1,0:T(8,128)S(1)}, f32[8,256]{1,0:T(8,128)S(1)}, u32[]{:S(2)}, u32[]{:S(2)}) collective-permute-start(f32[8,256]{1,0:T(8,128)S(1)} %get-tuple-element.15), channel_id=1, source_target_pairs={{0,28},{4,0},{8,4},{12,8},{16,12},{20,16},{24,20},{28,24},{1,29},{... | collective-permute-start | bytes 24584 | tf_op jit(solution)/shard_map/ppermute | solution.py:520
  81.1 6.2 %collective-permute-start.11 = (f32[8,256]{1,0:T(8,128)S(1)}, f32[8,256]{1,0:T(8,128)S(1)}, u32[]{:S(2)}, u32[]{:S(2)}) collective-permute-start(f32[8,256]{1,0:T(8,128)S(1)} %get-tuple-element.15), channel_id=1, source_target_pairs={{0,4},{4,8},{8,12},{12,16},{16,20},{20,24},{24,28},{28,0},{1,5},{5... | collective-permute-start | bytes 24584 | tf_op jit(solution)/shard_map/ppermute | solution.py:520
  83.1 4.2 %collective-permute-start.10 = (f32[8,256]{1,0:T(8,128)S(1)}, f32[8,256]{1,0:T(8,128)S(1)}, u32[]{:S(2)}, u32[]{:S(2)}) collective-permute-start(f32[8,256]{1,0:T(8,128)S(1)} %get-tuple-element.15), channel_id=1, source_target_pairs={{0,224},{32,0},{64,32},{96,64},{128,96},{160,128},{192,160},{224,1... | collective-permute-start | bytes 24584 | tf_op jit(solution)/shard_map/ppermute | solution.py:520
  83.3 4.1 %collective-permute-start.9 = (f32[8,256]{1,0:T(8,128)S(1)}, f32[8,256]{1,0:T(8,128)S(1)}, u32[]{:S(2)}, u32[]{:S(2)}) collective-permute-start(f32[8,256]{1,0:T(8,128)S(1)} %get-tuple-element.15), channel_id=1, source_target_pairs={{0,32},{32,64},{64,96},{96,128},{128,160},{160,192},{192,224},{224... | collective-permute-start | bytes 24584 | tf_op jit(solution)/shard_map/ppermute | solution.py:520
  (20 other events, 84.6 us)

commit v2 on v1

--- a/solution.py
+++ b/solution.py
@@ -106,25 +106,34 @@
     return after - before
 
 
-def arrange_kernel(weight, out):
-    for t in range(SLAB // LN):
-        out[t, 0:NF, :] = weight[:, t * LN : (t + 1) * LN]
-        out[t, NF : NF + 1, :] = jnp.zeros((1, LN), f32)
-
-
-def arrange(weight):
-    steps = weight.shape[1] // SLAB
+def arrange_kernel(meta, weight, out):
+    for n in range(weight.shape[2]):
+
+        @pl.when(meta[0] == n)
+        def _():
+            for t in range(SLAB // LN):
+                for a in range(NF):
+                    out[t, a : a + 1, :] = weight[0, a, n : n + 1, t * LN : (t + 1) * LN]
+
+    out[:, NF : NF + 1, :] = jnp.zeros((SLAB // LN, 1, LN), f32)
+
+
+def arrange(meta, weight):
+    steps = weight.shape[3] // SLAB
     per = SLAB // LN
     return pl.pallas_call(
         arrange_kernel,
         out_shape=shaped(steps * per, NF + 1, LN),
         grid=(steps,),
-        in_specs=[pl.BlockSpec((NF, SLAB), lambda s: (0, s))],
+        in_specs=[
+            pl.BlockSpec(memory_space=pltpu.SMEM),
+            pl.BlockSpec((1, NF, weight.shape[2], SLAB), lambda s: (0, 0, 0, s)),
+        ],
         out_specs=pl.BlockSpec((per, NF + 1, LN), lambda s: (s, 0, 0)),
         compiler_params=limit(8),
         cost_estimate=cost(1),
         name="arrange",
-    )(weight)
+    )(meta, weight)
 
 
 def lookup_kernel(meta, cell, height, out, high_low):
@@ -214,8 +223,8 @@
 
 
 def predict_kernel(
-    state, jacobians, stiffness, projection, send, east, north, integral, trace, sent,
-    spread, dof, coupled, pad, index,
+    state, jacobians, stiffness, projection, send, east, north, base, trace, sent,
+    spread, dof, coupled, pad, index, integral,
 ):
     spread_jacobians(jacobians, spread)
     coupled[...] = jnp.zeros((LN, EL), f32)
@@ -255,6 +264,11 @@
     sent[1:2, EL:] = east[TILE - 1 : TILE, :]
     sent[2:3, EL:] = as_row(north[:, 0:1])
     sent[3:4, EL:] = as_row(north[:, TILE - 1 : TILE])
+    couple(spread, integral, coupled)
+    volume = dot3(stiffness_rows(stiffness, pad, True), coupled[...])
+    base[...] = volume
+    for q in range(NQ):
+        base[0:NB, q * LN : (q + 1) * LN] = volume[0:NB, q * LN : (q + 1) * LN] + state[q]
 
 
 def predict(state, jacobians, stiffness, projection, send, east, north):
@@ -267,9 +281,10 @@
             pltpu.VMEM((LN, EL), f32),
             pltpu.VMEM((LN, LN), f32),
             pltpu.VMEM((8, LN), jnp.int32),
+            pltpu.VMEM((40, EL), f32),
         ],
         compiler_params=limit(24),
-        cost_estimate=cost(5),
+        cost_estimate=cost(4),
         name="predict",
     )(state, jacobians, stiffness, projection, send, east, north)
 
@@ -295,31 +310,6 @@
         cost_estimate=cost(2),
         name="uplift",
     )(inbound, trace, floor, heights)
-
-
-def volume_kernel(state, jacobians, stiffness, integral, base, spread, coupled, pad):
-    spread_jacobians(jacobians, spread)
-    coupled[...] = jnp.zeros((LN, EL), f32)
-    couple(spread, integral, coupled)
-    volume = dot3(stiffness_rows(stiffness, pad, True), coupled[...])
-    base[...] = volume
-    for q in range(NQ):
-        base[0:NB, q * LN : (q + 1) * LN] = volume[0:NB, q * LN : (q + 1) * LN] + state[q]
-
-
-def volume(state, jacobians, stiffness, integral):
-    return pl.pallas_call(
-        volume_kernel,
-        out_shape=shaped(40, EL),
-        scratch_shapes=[
-            pltpu.VMEM((243 * 8, LN), f32),
-            pltpu.VMEM((LN, EL), f32),
-            pltpu.VMEM((LN, LN), f32),
-        ],
-        compiler_params=limit(16),
-        cost_estimate=cost(3),
-        name="volume",
-    )(state, jacobians, stiffness, integral)
 
 
 def pressure_kernel(inbound, landed, floor, load, left, right):
@@ -420,8 +410,7 @@
 
 def ocean_kernel(
     meta, first, second, third, fourth, cell, below_x, above_x, below_y, above_y,
-    height, east, north, depth, new_height, edges,
-    left_a, right_a, left_b, right_b, total, lifts,
+    height, east, north, depth, new_height, edges, total, lifts,
 ):
     layers = meta[3]
     per = first.shape[0]
@@ -431,27 +420,24 @@
         layer = lax.rem(meta[0] - shift + layers, layers)
         lifts[pl.ds(pl.multiple_of(layer * per, 8), per)] = values[:, 0, :]
 
-    def build(c, left, right):
+    def chunk(c, carry):
         for half in range(2):
             t = c * 2 + half
             cells = cell[0, :, pl.ds(pl.multiple_of(t * LN, LN), LN)]
-            for layer in range(4):
-                here = cells[layer : layer + 1, :]
-                value = jnp.broadcast_to(lifts[pl.ds(layer * per + t, 1), :], (16, LN))
-                high, low = one_hot(here >> 8, TILE, split(value))
-                left[half * 4 + layer, 0:TILE] = high
-                left[half * 4 + layer, TILE:] = low
-                (right[half * 4 + layer],) = one_hot(here & 255, TILE, [one])
-
-    def chunks(c, carry):
-        build(2 * c + 1, left_b, right_b)
-        total[...] += joined(left_a, right_a)
-        build(jnp.minimum(2 * c + 2, per // 2 - 1), left_a, right_a)
-        total[...] += joined(left_b, right_b)
+            for pair in range(2):
+                left, right = [], []
+                for layer in (2 * pair, 2 * pair + 1):
+                    here = cells[layer : layer + 1, :]
+                    value = jnp.broadcast_to(lifts[pl.ds(layer * per + t, 1), :], (16, LN))
+                    left.append(jnp.concatenate(one_hot(here >> 8, TILE, split(value)), axis=0))
+                    right += one_hot(here & 255, TILE, [one])
+                total[...] += lax.dot_general(
+                    jnp.concatenate(left, axis=1), jnp.concatenate(right, axis=1), NT,
+                    preferred_element_type=f32,
+                )
         return carry
 
-    build(0, left_a, right_a)
-    lax.fori_loop(0, per // 4, chunks, 0)
+    lax.fori_loop(0, per // 2, chunk, 0, unroll=8)
     source = total[0:TILE] + total[TILE:]
     rim = slice(EL, EDGE)
     low_x = jnp.where(meta[1] > 0, below_x[1:2, rim], 0.0)
@@ -478,10 +464,6 @@
         in_specs=[smem] + [vmem] * 13,
         out_specs=(vmem, vmem),
         scratch_shapes=[
-            pltpu.VMEM((8, 2 * TILE, LN), bf16),
-            pltpu.VMEM((8, TILE, LN), bf16),
-            pltpu.VMEM((8, 2 * TILE, LN), bf16),
-            pltpu.VMEM((8, TILE, LN), bf16),
             pltpu.VMEM((2 * TILE, TILE), f32),
             pltpu.VMEM((4 * layers[0].shape[0], LN), f32),
         ],
@@ -550,17 +532,18 @@
         jnp.transpose(x, (1, 2, 0, 3)) for x in (jacobians, flux_self, flux_other)
     )
     projection = jnp.transpose(projection, (1, 0, 2))
-    weight = lax.dynamic_index_in_dim(ocean_weight[0], lax.axis_index("gz"), 0, keepdims=False)
-    inbound = lax.all_to_all(arrange(weight), ("gx", "gy"), 0, 0, tiled=True)
-    integral, trace, sent = predict(
+    weight = jnp.transpose(ocean_weight, (0, 2, 1, 3))
+    inbound = lax.all_to_all(arrange(meta, weight), ("gx", "gy"), 0, 0, tiled=True)
+    base, trace, sent = predict(
         element_state, jacobians, stiffness, projection, send_faces, east_flow, north_flow
     )
     heights = lookup(meta, ocean_cell, height)
+    early = [shifted(sent, "gz", step) for step in (1, -1)]
+    inbound, *early = lax.optimization_barrier((inbound, *early))
     lifted = uplift(inbound, trace, floor, heights)
     landed = lax.all_to_all(lifted, ("gx", "gy"), 0, 0, tiled=True)
-    received = [shifted(sent, axis, step) for axis in ("gx", "gy", "gz") for step in (1, -1)]
+    received = [shifted(sent, axis, step) for axis in ("gx", "gy") for step in (1, -1)] + early
     layers = [landed] + [shifted(landed, "gz", step) for step in (1, 2, 3)]
-    base = volume(element_state, jacobians, stiffness, integral)
     load = pressure(inbound, landed, floor)
     new_height, edges = ocean(
         meta, layers, ocean_cell, received, height, east_flow, north_flow, water_depth

time: 90.4 us -> 83.8 us (0.927); the launches traced: 88.9 us -> 83.5 us
  local copies, waits for them, and re-layouts: 9.82 us -> 1.62 us
  waiting for transfers between devices: 7.49 us -> 11.6 us
  Pallas kernels: 34.6 us -> 31 us
  starting transfers between devices: 36 us -> 38.3 us
    unnamed x59 -> x34, local copies, waits for them, and re-layouts: 9.27 us -> 1.62 us
    pallas_call x1, Pallas kernels: 15.1 us -> 11.2 us  [ocean(): pl.pallas_call(ocean_kernel, out_shape=(shaped(TILE, TILE), shaped(8, TIL...]
    ppermute x13, starting transfers between devices: 16.6 us -> 18.8 us  [shifted(): lax.ppermute(value, axis, [(i, (i + step) % count) for i in range(count)])]
    ppermute x13, waiting for transfers between devices: 0.03 us -> 2.12 us  [shifted(): lax.ppermute(value, axis, [(i, (i + step) % count) for i in range(count)])]
    all_to_all x1, waiting for transfers between devices: 2.35 us -> 4.38 us  [on_device(): landed = lax.all_to_all(lifted, ('gx', 'gy'), 0, 0, tiled=True)]
    pallas_call x1, Pallas kernels: 2.63 us -> 3.57 us  [arrange(): pl.pallas_call(arrange_kernel, out_shape=shaped(steps * per, NF + 1, LN),...]
  transfers between devices with their start and end apart: 15 -> 15, of which waited for: 2 -> 3; matrix products, arithmetic and copies ran while one was open for 0% -> 0% of each run, Pallas kernels for 32% -> 15%
where the time goes in v2:
time: 83.8 us; the launch traced here: 83.5 us
  starting transfers between devices  38.3 us (46%)
  Pallas kernels  31 us (37%)
  waiting for transfers between devices  11.6 us (14%)
  local copies, waits for them, and re-layouts  1.62 us (2%)
  between operations  0.92 us (1%)
    ppermute x13, starting transfers between devices, shifted(): lax.ppermute(value, axis, [(i, (i + step) % count) for i in range(count)])  18.8 us
    all_to_all x1, starting transfers between devices, on_device(): lax.all_to_all(arrange(meta, weight), ('gx', 'gy'), 0, 0, tiled=True)  12.4 us
    pallas_call x1, Pallas kernels, ocean(): pl.pallas_call(ocean_kernel, out_shape=(shaped(TILE, TILE), shaped(8, TIL...  11.2 us
    all_to_all x1, starting transfers between devices, on_device(): landed = lax.all_to_all(lifted, ('gx', 'gy'), 0, 0, tiled=True)  7.18 us
    all_to_all x1, waiting for transfers between devices, on_device(): lax.all_to_all(arrange(meta, weight), ('gx', 'gy'), 0, 0, tiled=True)  5.14 us
    all_to_all x1, waiting for transfers between devices, on_device(): landed = lax.all_to_all(lifted, ('gx', 'gy'), 0, 0, tiled=True)  4.38 us
    pallas_call x1, Pallas kernels, lookup(): pl.pallas_call(lookup_kernel, out_shape=shaped(ocean_cell.shape[2] // LN,...  4.24 us
    pallas_call x1, Pallas kernels, predict(): pl.pallas_call(predict_kernel, out_shape=(shaped(40, EL), shaped(64, EL),...  3.78 us
  transfers between devices with their start and end apart: 15, of which 3 were waited for; matrix products, arithmetic and copies ran while one was open for 0% of the time, Pallas kernels for 15%

profile of v2, /device:TPU:7, one launch (start us, length us, event | category | flops | bytes accessed | tf_op | source)
XLA Modules:
  0.0 83.5 jit_solution(13931118560205731634)
XLA Ops:
  0.7 1.5 %copy-done = f32[1,4,15,8192]{3,1,2,0:T(4,128)S(1)} copy-done((f32[1,4,15,8192]{3,1,2,0:T(4,128)S(1)}, f32[1,4,15,8192]{3,1,2,0:T(4,128)}, u32[]{:S(2)}) %copy-start) | copy-done | bytes 1966104
  2.2 3.6 %arrange.1 = f32[64,16,128]{2,1,0:T(8,128)} custom-call(s32[8]{0:T(128)S(1)} %compare_select_fusion.5.meta, f32[1,15,4,8192]{3,2,1,0:T(4,128)S(1)} %bitcast.7), custom_call_target="tpu_custom_call" | custom-call | flops 200000000 | bytes 1048576 | tf_op jit(solution)/shard_map/arrange/pallas_call | solution.py:124
  5.8 12.4 %all-to-all-start = ((f32[64,16,128]{2,1,0:T(8,128)}), f32[64,16,128]{2,1,0:T(8,128)S(1)}, u32[]{:S(2)}, u32[]{:S(2)}) async-start(f32[64,16,128]{2,1,0:T(8,128)} %arrange.1), calls=%async_computation | async-start | bytes 1048576 | tf_op jit(solution)/shard_map/all_to_all | solution.py:536
  18.3 3.8 %predict.1 = (f32[40,1152]{1,0:T(8,128)S(1)}, f32[64,1152]{1,0:T(8,128)S(1)}, f32[16,1408]{1,0:T(8,128)S(1)}) custom-call(f32[9,35,128]{2,1,0:T(8,128)S(1)} %copy-done.5, f32[9,9,3,128]{3,2,1,0:T(4,128)S(1)} %bitcast.8, f32[3,35,35]{2,1,0:T(8,128)S(1)} %copy-done.10, f32[15,4,35]{2,1,0:T(4,128)S(1)} %bitcast.13, s32[6,16]{1,0:T(8,128)S(1)} %copy-done.13, ...), custom_call_target="tpu_custom_call" | custom-call | flops 800000000 | bytes 1048576 | tf_op jit(solution)/shard_map/predict/pallas_call | solution.py:275
  22.1 1.4 %collective-permute-start = (f32[16,1408]{1,0:T(8,128)S(1)}, f32[16,1408]{1,0:T(8,128)S(1)}, u32[]{:S(2)}, u32[]{:S(2)}) collective-permute-start(f32[16,1408]{1,0:T(8,128)S(1)} %get-tuple-element.15), channel_id=1, source_target_pairs={{0,1},{1,2},{2,3},{3,0},{4,5},{5,6},{6,7},{7,4},{8,9},{9,10},{10,1... | collective-permute-start | bytes 270344 | tf_op jit(solution)/shard_map/ppermute | solution.py:502
  23.4 1.5 %collective-permute-start.1 = (f32[16,1408]{1,0:T(8,128)S(1)}, f32[16,1408]{1,0:T(8,128)S(1)}, u32[]{:S(2)}, u32[]{:S(2)}) collective-permute-start(f32[16,1408]{1,0:T(8,128)S(1)} %get-tuple-element.15), channel_id=1, source_target_pairs={{0,3},{1,0},{2,1},{3,2},{4,7},{5,4},{6,5},{7,6},{8,11},{9,8},{10,9... | collective-permute-start | bytes 270344 | tf_op jit(solution)/shard_map/ppermute | solution.py:502
  25.0 4.2 %lookup.1.heights = f32[64,128]{1,0:T(8,128)S(1)} custom-call(s32[8]{0:T(128)S(1)} %compare_select_fusion.5.meta, s32[1,4,8192]{2,1,0:T(4,128)S(1)} %copy-done.9, f32[256,256]{1,0:T(8,128)S(1)} %copy-done.1), custom_call_target="tpu_custom_call" | custom-call | flops 1200000000 | bytes 1048576 | tf_op jit(solution)/shard_map/lookup/pallas_call | solution.py:169
  29.3 5.1 %all-to-all-done.inbound = f32[64,16,128]{2,1,0:T(8,128)S(1)} async-done(((f32[64,16,128]{2,1,0:T(8,128)}), f32[64,16,128]{2,1,0:T(8,128)S(1)}, u32[]{:S(2)}, u32[]{:S(2)}) %all-to-all-start) | async-done | bytes 524320 | tf_op jit(solution)/shard_map/all_to_all | solution.py:536
  34.4 2.2 %uplift.1 = f32[64,2,128]{2,1,0:T(2,128)} custom-call(f32[64,16,128]{2,1,0:T(8,128)S(1)} %all-to-all-done.inbound, f32[64,1152]{1,0:T(8,128)S(1)} %get-tuple-element.17.trace, s32[64,128]{1,0:T(8,128)S(1)} %bitcast.11, f32[64,128]{1,0:T(8,128)S(1)} %lookup.1.heights), custom_call_target="tpu_custom_call" | custom-call | flops 400000000 | bytes 1048576 | tf_op jit(solution)/shard_map/uplift/pallas_call | solution.py:306
  36.6 7.2 %all-to-all-start.1 = ((f32[64,2,128]{2,1,0:T(2,128)}), f32[64,2,128]{2,1,0:T(2,128)S(1)}, u32[]{:S(2)}, u32[]{:S(2)}) async-start(f32[64,2,128]{2,1,0:T(2,128)} %uplift.1), calls=%async_computation.1 | async-start | bytes 131072 | tf_op jit(solution)/shard_map/all_to_all | solution.py:544
  43.8 1.3 %collective-permute-start.2 = (f32[16,1408]{1,0:T(8,128)S(1)}, f32[16,1408]{1,0:T(8,128)S(1)}, u32[]{:S(2)}, u32[]{:S(2)}) collective-permute-start(f32[16,1408]{1,0:T(8,128)S(1)} %get-tuple-element.15), channel_id=1, source_target_pairs={{0,32},{32,64},{64,96},{96,128},{128,160},{160,192},{192,224},{224... | collective-permute-start | bytes 270344 | tf_op jit(solution)/shard_map/ppermute | solution.py:502
  45.0 1.6 %collective-permute-start.3 = (f32[16,1408]{1,0:T(8,128)S(1)}, f32[16,1408]{1,0:T(8,128)S(1)}, u32[]{:S(2)}, u32[]{:S(2)}) collective-permute-start(f32[16,1408]{1,0:T(8,128)S(1)} %get-tuple-element.15), channel_id=1, source_target_pairs={{0,224},{32,0},{64,32},{96,64},{128,96},{160,128},{192,160},{224,1... | collective-permute-start | bytes 270344 | tf_op jit(solution)/shard_map/ppermute | solution.py:502
  46.6 0.9 %collective-permute-start.4 = (f32[16,1408]{1,0:T(8,128)S(1)}, f32[16,1408]{1,0:T(8,128)S(1)}, u32[]{:S(2)}, u32[]{:S(2)}) collective-permute-start(f32[16,1408]{1,0:T(8,128)S(1)} %get-tuple-element.15), channel_id=1, source_target_pairs={{0,4},{4,8},{8,12},{12,16},{16,20},{20,24},{24,28},{28,0},{1,5},{5... | collective-permute-start | bytes 270344 | tf_op jit(solution)/shard_map/ppermute | solution.py:502
  47.6 4.4 %all-to-all-done.1.landed.first = f32[64,2,128]{2,1,0:T(2,128)S(1)} async-done(((f32[64,2,128]{2,1,0:T(2,128)}), f32[64,2,128]{2,1,0:T(2,128)S(1)}, u32[]{:S(2)}, u32[]{:S(2)}) %all-to-all-start.1) | async-done | bytes 65568 | tf_op jit(solution)/shard_map/all_to_all | solution.py:544
  51.9 1.3 %collective-permute-start.6 = (f32[64,2,128]{2,1,0:T(2,128)S(1)}, f32[64,2,128]{2,1,0:T(2,128)S(1)}, u32[]{:S(2)}, u32[]{:S(2)}) collective-permute-start(f32[64,2,128]{2,1,0:T(2,128)S(1)} %all-to-all-done.1.landed.first), channel_id=1, source_target_pairs={{0,1},{1,2},{2,3},{3,0},{4,5},{5,6},{6,7},{7,4},{8,9},{9,10},{10,1... | collective-permute-start | bytes 196616 | tf_op jit(solution)/shard_map/ppermute | solution.py:502
  53.2 2.6 %collective-permute-start.7 = (f32[64,2,128]{2,1,0:T(2,128)S(1)}, f32[64,2,128]{2,1,0:T(2,128)S(1)}, u32[]{:S(2)}, u32[]{:S(2)}) collective-permute-start(f32[64,2,128]{2,1,0:T(2,128)S(1)} %all-to-all-done.1.landed.first), channel_id=1, source_target_pairs={{0,2},{1,3},{2,0},{3,1},{4,6},{5,7},{6,4},{7,5},{8,10},{9,11},{10,... | collective-permute-start | bytes 196616 | tf_op jit(solution)/shard_map/ppermute | solution.py:502
  55.9 1.1 %collective-permute-start.8 = (f32[64,2,128]{2,1,0:T(2,128)S(1)}, f32[64,2,128]{2,1,0:T(2,128)S(1)}, u32[]{:S(2)}, u32[]{:S(2)}) collective-permute-start(f32[64,2,128]{2,1,0:T(2,128)S(1)} %all-to-all-done.1.landed.first), channel_id=1, source_target_pairs={{0,3},{1,0},{2,1},{3,2},{4,7},{5,4},{6,5},{7,6},{8,11},{9,8},{10,9... | collective-permute-start | bytes 196616 | tf_op jit(solution)/shard_map/ppermute | solution.py:502
  56.9 2.3 %pressure.1.load = f32[64,128]{1,0:T(8,128)S(1)} custom-call(f32[64,16,128]{2,1,0:T(8,128)S(1)} %all-to-all-done.inbound, f32[64,2,128]{2,1,0:T(2,128)S(1)} %all-to-all-done.1.landed.first, s32[64,128]{1,0:T(8,128)S(1)} %bitcast.12), custom_call_target="tpu_custom_call" | custom-call | flops 600000000 | bytes 1048576 | tf_op jit(solution)/shard_map/pressure/pallas_call | solution.py:337
  59.4 11.2 %ocean.1 = (f32[256,256]{1,0:T(8,128)}, f32[8,256]{1,0:T(8,128)S(1)}) custom-call(s32[8]{0:T(128)S(1)} %compare_select_fusion.5.meta, f32[64,2,128]{2,1,0:T(2,128)S(1)} %all-to-all-done.1.landed.first, f32[64,2,128]{2,1,0:T(2,128)S(1)} %collective-permute-done.6.second, f32[64,2,128]{2,1,0:T(2,128)S(1)} %collective-permute-done.7.third, ...), custom_call_target="tpu_custom_call" | custom-call | flops 2000000000 | bytes 1048576 | tf_op jit(solution)/shard_map/ocean/pallas_call | solution.py:461
  70.9 2.4 %collective-permute-start.10 = (f32[8,256]{1,0:T(8,128)S(1)}, f32[8,256]{1,0:T(8,128)S(1)}, u32[]{:S(2)}, u32[]{:S(2)}) collective-permute-start(f32[8,256]{1,0:T(8,128)S(1)} %get-tuple-element.21), channel_id=1, source_target_pairs={{0,224},{32,0},{64,32},{96,64},{128,96},{160,128},{192,160},{224,1... | collective-permute-start | bytes 24584 | tf_op jit(solution)/shard_map/ppermute | solution.py:502
  73.3 4.4 %collective-permute-start.11 = (f32[8,256]{1,0:T(8,128)S(1)}, f32[8,256]{1,0:T(8,128)S(1)}, u32[]{:S(2)}, u32[]{:S(2)}) collective-permute-start(f32[8,256]{1,0:T(8,128)S(1)} %get-tuple-element.21), channel_id=1, source_target_pairs={{0,4},{4,8},{8,12},{12,16},{16,20},{20,24},{24,28},{28,0},{1,5},{5... | collective-permute-start | bytes 24584 | tf_op jit(solution)/shard_map/ppermute | solution.py:502
  77.7 2.2 %flux.1 = f32[9,35,128]{2,1,0:T(8,128)} custom-call(s32[8]{0:T(128)S(1)} %compare_select_fusion.5.meta, f32[9,35,128]{2,1,0:T(8,128)S(1)} %copy-done.5, f32[40,1152]{1,0:T(8,128)S(1)} %get-tuple-element.14.base, f32[64,128]{1,0:T(8,128)S(1)} %pressure.1.load, f32[64,1152]{1,0:T(8,128)S(1)} %get-tuple-element.17.trace, ...), custom_call_target="tpu_custom_call" | custom-call | flops 800000000 | bytes 1048576 | tf_op jit(solution)/shard_map/flux/pallas_call | solution.py:395
  79.9 2.1 %collective-permute-done.12.above_y = f32[8,256]{1,0:T(8,128)S(1)} collective-permute-done((f32[8,256]{1,0:T(8,128)S(1)}, f32[8,256]{1,0:T(8,128)S(1)}, u32[]{:S(2)}, u32[]{:S(2)}) %collective-permute-start.12) | collective-permute-done | bytes 8224 | tf_op jit(solution)/shard_map/ppermute | solution.py:502
  82.0 1.6 %flow.1 = (f32[256,256]{1,0:T(8,128)}, f32[256,256]{1,0:T(8,128)}) custom-call(s32[8]{0:T(128)S(1)} %compare_select_fusion.5.meta, f32[256,256]{1,0:T(8,128)S(1)} %copy-done.16, f32[256,256]{1,0:T(8,128)S(1)} %copy-done.3, f32[256,256]{1,0:T(8,128)S(1)} %copy-done.4, f32[8,256]{1,0:T(8,128)S(1)} %collective-permute-done.9.below_x, ...), custom_call_target="tpu_custom_call" | custom-call | flops 400000000 | bytes 1048576 | tf_op jit(solution)/shard_map/flow/pallas_call | solution.py:489
  (49 shorter events, 0.4 us)
Async XLA Ops:
  0.6 17.6 %copy-start.13 = (s32[6,16]{1,0:T(8,128)S(1)}, s32[6,16]{1,0:T(8,128)}, u32[]{:S(2)}) copy-start(s32[6,16]{1,0:T(8,128)} %send.1) | copy-start | bytes 1156
  2.2 16.0 %copy-start.10 = (f32[3,35,35]{2,1,0:T(8,128)S(1)}, f32[3,35,35]{2,1,0:T(8,128)}, u32[]{:S(2)}) copy-start(f32[3,35,35]{2,1,0:T(8,128)} %stiffness.1) | copy-start | bytes 44104
  5.8 19.2 %copy-start.1 = (f32[256,256]{1,0:T(8,128)S(1)}, f32[256,256]{1,0:T(8,128)}, u32[]{:S(2)}) copy-start(f32[256,256]{1,0:T(8,128)} %height.3) | copy-start | bytes 786436
  5.8 19.2 %copy-start.9 = (s32[1,4,8192]{2,1,0:T(4,128)S(1)}, s32[1,4,8192]{2,1,0:T(4,128)}, u32[]{:S(2)}) copy-start(s32[1,4,8192]{2,1,0:T(4,128)} %cell.3) | copy-start | bytes 393220
  5.8 28.6 %all-to-all-start = ((f32[64,16,128]{2,1,0:T(8,128)}), f32[64,16,128]{2,1,0:T(8,128)S(1)}, u32[]{:S(2)}, u32[]{:S(2)}) async-start(f32[64,16,128]{2,1,0:T(8,128)} %arrange.1), calls=%async_computation | async-start | bytes 1048576 | tf_op jit(solution)/shard_map/all_to_all | solution.py:536
  22.1 7.2 %collective-permute-start = (f32[16,1408]{1,0:T(8,128)S(1)}, f32[16,1408]{1,0:T(8,128)S(1)}, u32[]{:S(2)}, u32[]{:S(2)}) collective-permute-start(f32[16,1408]{1,0:T(8,128)S(1)} %get-tuple-element.15), channel_id=1, source_target_pairs={{0,1},{1,2},{2,3},{3,0},{4,5},{5,6},{6,7},{7,4},{8,9},{9,10},{10,1... | collective-permute-start | bytes 270344 | tf_op jit(solution)/shard_map/ppermute | solution.py:502
  23.4 5.8 %collective-permute-start.1 = (f32[16,1408]{1,0:T(8,128)S(1)}, f32[16,1408]{1,0:T(8,128)S(1)}, u32[]{:S(2)}, u32[]{:S(2)}) collective-permute-start(f32[16,1408]{1,0:T(8,128)S(1)} %get-tuple-element.15), channel_id=1, source_target_pairs={{0,3},{1,0},{2,1},{3,2},{4,7},{5,4},{6,5},{7,6},{8,11},{9,8},{10,9... | collective-permute-start | bytes 270344 | tf_op jit(solution)/shard_map/ppermute | solution.py:502
  29.2 30.1 %copy-start.2 = (f32[256,256]{1,0:T(8,128)S(1)}, f32[256,256]{1,0:T(8,128)}, u32[]{:S(2)}) copy-start(f32[256,256]{1,0:T(8,128)} %depth.1) | copy-start | bytes 786436
  36.6 15.3 %all-to-all-start.1 = ((f32[64,2,128]{2,1,0:T(2,128)}), f32[64,2,128]{2,1,0:T(2,128)S(1)}, u32[]{:S(2)}, u32[]{:S(2)}) async-start(f32[64,2,128]{2,1,0:T(2,128)} %uplift.1), calls=%async_computation.1 | async-start | bytes 131072 | tf_op jit(solution)/shard_map/all_to_all | solution.py:544
  43.8 9.5 %collective-permute-start.2 = (f32[16,1408]{1,0:T(8,128)S(1)}, f32[16,1408]{1,0:T(8,128)S(1)}, u32[]{:S(2)}, u32[]{:S(2)}) collective-permute-start(f32[16,1408]{1,0:T(8,128)S(1)} %get-tuple-element.15), channel_id=1, source_target_pairs={{0,32},{32,64},{64,96},{96,128},{128,160},{160,192},{192,224},{224... | collective-permute-start | bytes 270344 | tf_op jit(solution)/shard_map/ppermute | solution.py:502
  45.0 10.8 %collective-permute-start.3 = (f32[16,1408]{1,0:T(8,128)S(1)}, f32[16,1408]{1,0:T(8,128)S(1)}, u32[]{:S(2)}, u32[]{:S(2)}) collective-permute-start(f32[16,1408]{1,0:T(8,128)S(1)} %get-tuple-element.15), channel_id=1, source_target_pairs={{0,224},{32,0},{64,32},{96,64},{128,96},{160,128},{192,160},{224,1... | collective-permute-start | bytes 270344 | tf_op jit(solution)/shard_map/ppermute | solution.py:502
  46.6 12.7 %collective-permute-start.4 = (f32[16,1408]{1,0:T(8,128)S(1)}, f32[16,1408]{1,0:T(8,128)S(1)}, u32[]{:S(2)}, u32[]{:S(2)}) collective-permute-start(f32[16,1408]{1,0:T(8,128)S(1)} %get-tuple-element.15), channel_id=1, source_target_pairs={{0,4},{4,8},{8,12},{12,16},{16,20},{20,24},{24,28},{28,0},{1,5},{5... | collective-permute-start | bytes 270344 | tf_op jit(solution)/shard_map/ppermute | solution.py:502
  47.5 11.8 %collective-permute-start.5 = (f32[16,1408]{1,0:T(8,128)S(1)}, f32[16,1408]{1,0:T(8,128)S(1)}, u32[]{:S(2)}, u32[]{:S(2)}) collective-permute-start(f32[16,1408]{1,0:T(8,128)S(1)} %get-tuple-element.15), channel_id=1, source_target_pairs={{0,28},{4,0},{8,4},{12,8},{16,12},{20,16},{24,20},{28,24},{1,29},{... | collective-permute-start | bytes 270344 | tf_op jit(solution)/shard_map/ppermute | solution.py:502
  51.9 7.4 %collective-permute-start.6 = (f32[64,2,128]{2,1,0:T(2,128)S(1)}, f32[64,2,128]{2,1,0:T(2,128)S(1)}, u32[]{:S(2)}, u32[]{:S(2)}) collective-permute-start(f32[64,2,128]{2,1,0:T(2,128)S(1)} %all-to-all-done.1.landed.first), channel_id=1, source_target_pairs={{0,1},{1,2},{2,3},{3,0},{4,5},{5,6},{6,7},{7,4},{8,9},{9,10},{10,1... | collective-permute-start | bytes 196616 | tf_op jit(solution)/shard_map/ppermute | solution.py:502
  53.2 6.1 %collective-permute-start.7 = (f32[64,2,128]{2,1,0:T(2,128)S(1)}, f32[64,2,128]{2,1,0:T(2,128)S(1)}, u32[]{:S(2)}, u32[]{:S(2)}) collective-permute-start(f32[64,2,128]{2,1,0:T(2,128)S(1)} %all-to-all-done.1.landed.first), channel_id=1, source_target_pairs={{0,2},{1,3},{2,0},{3,1},{4,6},{5,7},{6,4},{7,5},{8,10},{9,11},{10,... | collective-permute-start | bytes 196616 | tf_op jit(solution)/shard_map/ppermute | solution.py:502
  55.9 3.5 %collective-permute-start.8 = (f32[64,2,128]{2,1,0:T(2,128)S(1)}, f32[64,2,128]{2,1,0:T(2,128)S(1)}, u32[]{:S(2)}, u32[]{:S(2)}) collective-permute-start(f32[64,2,128]{2,1,0:T(2,128)S(1)} %all-to-all-done.1.landed.first), channel_id=1, source_target_pairs={{0,3},{1,0},{2,1},{3,2},{4,7},{5,4},{6,5},{7,6},{8,11},{9,8},{10,9... | collective-permute-start | bytes 196616 | tf_op jit(solution)/shard_map/ppermute | solution.py:502
  59.3 18.4 %copy-start.7 = (f32[4,9,9,128]{3,0,2,1:T(4,128)S(1)}, f32[4,9,9,128]{3,0,2,1:T(4,128)}, u32[]{:S(2)}) copy-start(f32[4,9,9,128]{3,0,2,1:T(4,128)} %param.20) | copy-start | bytes 497668
  59.3 18.4 %copy-start.8 = (f32[4,9,9,128]{3,0,2,1:T(4,128)S(1)}, f32[4,9,9,128]{3,0,2,1:T(4,128)}, u32[]{:S(2)}) copy-start(f32[4,9,9,128]{3,0,2,1:T(4,128)} %param.21) | copy-start | bytes 497668
  59.3 18.4 %copy-start.14 = (s32[4,128]{1,0:T(4,128)S(1)}, s32[4,128]{1,0:T(4,128)}, u32[]{:S(2)}) copy-start(s32[4,128]{1,0:T(4,128)} %source.1) | copy-start | bytes 6148
  59.3 18.4 %copy-start.15 = (s32[128]{0:T(128)S(1)}, s32[128]{0:T(128)}, u32[]{:S(2)}) copy-start(s32[128]{0:T(128)} %param.24) | copy-start | bytes 1540
  70.6 9.3 %collective-permute-start.9 = (f32[8,256]{1,0:T(8,128)S(1)}, f32[8,256]{1,0:T(8,128)S(1)}, u32[]{:S(2)}, u32[]{:S(2)}) collective-permute-start(f32[8,256]{1,0:T(8,128)S(1)} %get-tuple-element.21), channel_id=1, source_target_pairs={{0,32},{32,64},{64,96},{96,128},{128,160},{160,192},{192,224},{224... | collective-permute-start | bytes 24584 | tf_op jit(solution)/shard_map/ppermute | solution.py:502
  70.9 9.0 %collective-permute-start.10 = (f32[8,256]{1,0:T(8,128)S(1)}, f32[8,256]{1,0:T(8,128)S(1)}, u32[]{:S(2)}, u32[]{:S(2)}) collective-permute-start(f32[8,256]{1,0:T(8,128)S(1)} %get-tuple-element.21), channel_id=1, source_target_pairs={{0,224},{32,0},{64,32},{96,64},{128,96},{160,128},{192,160},{224,1... | collective-permute-start | bytes 24584 | tf_op jit(solution)/shard_map/ppermute | solution.py:502
  73.3 6.6 %collective-permute-start.11 = (f32[8,256]{1,0:T(8,128)S(1)}, f32[8,256]{1,0:T(8,128)S(1)}, u32[]{:S(2)}, u32[]{:S(2)}) collective-permute-start(f32[8,256]{1,0:T(8,128)S(1)} %get-tuple-element.21), channel_id=1, source_target_pairs={{0,4},{4,8},{8,12},{12,16},{16,20},{20,24},{24,28},{28,0},{1,5},{5... | collective-permute-start | bytes 24584 | tf_op jit(solution)/shard_map/ppermute | solution.py:502
  77.7 4.3 %collective-permute-start.12 = (f32[8,256]{1,0:T(8,128)S(1)}, f32[8,256]{1,0:T(8,128)S(1)}, u32[]{:S(2)}, u32[]{:S(2)}) collective-permute-start(f32[8,256]{1,0:T(8,128)S(1)} %get-tuple-element.21), channel_id=1, source_target_pairs={{0,28},{4,0},{8,4},{12,8},{16,12},{20,16},{24,20},{28,24},{1,29},{... | collective-permute-start | bytes 24584 | tf_op jit(solution)/shard_map/ppermute | solution.py:502
  (8 other events, 105.4 us)

commit v3 on v2

--- a/solution.py
+++ b/solution.py
@@ -12,6 +12,7 @@
 EL = NQ * LN
 TILE = 256
 SLAB = 1024
+WIDE = 2048
 EDGE = EL + TILE
 
 time_step = 1.5
@@ -111,26 +112,26 @@
 
         @pl.when(meta[0] == n)
         def _():
-            for t in range(SLAB // LN):
+            for t in range(WIDE // LN):
                 for a in range(NF):
                     out[t, a : a + 1, :] = weight[0, a, n : n + 1, t * LN : (t + 1) * LN]
 
-    out[:, NF : NF + 1, :] = jnp.zeros((SLAB // LN, 1, LN), f32)
+    out[:, NF : NF + 1, :] = jnp.zeros((WIDE // LN, 1, LN), f32)
 
 
 def arrange(meta, weight):
-    steps = weight.shape[3] // SLAB
-    per = SLAB // LN
+    steps = weight.shape[3] // WIDE
+    per = WIDE // LN
     return pl.pallas_call(
         arrange_kernel,
         out_shape=shaped(steps * per, NF + 1, LN),
         grid=(steps,),
         in_specs=[
             pl.BlockSpec(memory_space=pltpu.SMEM),
-            pl.BlockSpec((1, NF, weight.shape[2], SLAB), lambda s: (0, 0, 0, s)),
+            pl.BlockSpec((1, NF, weight.shape[2], WIDE), lambda s: (0, 0, 0, s)),
         ],
         out_specs=pl.BlockSpec((per, NF + 1, LN), lambda s: (s, 0, 0)),
-        compiler_params=limit(8),
+        compiler_params=limit(60),
         cost_estimate=cost(1),
         name="arrange",
     )(meta, weight)
@@ -289,27 +290,41 @@
     )(state, jacobians, stiffness, projection, send, east, north)
 
 
-def uplift_kernel(inbound, trace, floor, heights, out):
+def choose_kernel(trace, floor, out):
     def tile(r, carry):
         face = jnp.broadcast_to(floor[pl.ds(r, 1), :], (16, LN))
-        found = pick(
+        out[r] = pick(
             lambda s: trace[s * 16 : (s + 1) * 16, 8 * LN : 9 * LN], face & 127, face >> 7, 4
         )
-        out[r, 0:1, :] = jnp.sum(inbound[r] * found, axis=0, keepdims=True)
-        out[r, 1:2, :] = heights[pl.ds(r, 1), :]
         return carry
 
     lax.fori_loop(0, floor.shape[0], tile, 0, unroll=8)
 
 
-def uplift(inbound, trace, floor, heights):
-    return pl.pallas_call(
-        uplift_kernel,
-        out_shape=shaped(floor.shape[0], 2, LN),
+def choose(trace, floor):
+    return pl.pallas_call(
+        choose_kernel,
+        out_shape=shaped(floor.shape[0], NF + 1, LN),
         compiler_params=limit(16),
         cost_estimate=cost(2),
+        name="choose",
+    )(trace, floor)
+
+
+def uplift_kernel(inbound, chosen, heights, out):
+    for r in range(heights.shape[0]):
+        out[r, 0:1, :] = jnp.sum(inbound[r] * chosen[r], axis=0, keepdims=True)
+        out[r, 1:2, :] = heights[r : r + 1, :]
+
+
+def uplift(inbound, chosen, heights):
+    return pl.pallas_call(
+        uplift_kernel,
+        out_shape=shaped(heights.shape[0], 2, LN),
+        compiler_params=limit(16),
+        cost_estimate=cost(1),
         name="uplift",
-    )(inbound, trace, floor, heights)
+    )(inbound, chosen, heights)
 
 
 def pressure_kernel(inbound, landed, floor, load, left, right):
@@ -539,8 +554,9 @@
     )
     heights = lookup(meta, ocean_cell, height)
     early = [shifted(sent, "gz", step) for step in (1, -1)]
-    inbound, *early = lax.optimization_barrier((inbound, *early))
-    lifted = uplift(inbound, trace, floor, heights)
+    chosen = choose(trace, floor)
+    inbound, chosen, heights, *early = lax.optimization_barrier((inbound, chosen, heights, *early))
+    lifted = uplift(inbound, chosen, heights)
     landed = lax.all_to_all(lifted, ("gx", "gy"), 0, 0, tiled=True)
     received = [shifted(sent, axis, step) for axis in ("gx", "gy") for step in (1, -1)] + early
     layers = [landed] + [shifted(landed, "gz", step) for step in (1, 2, 3)]

time: 83.8 us -> 81.5 us (0.973)
  local copies, waits for them, and re-layouts: 1.62 us -> 0.09 us
  waiting for transfers between devices: 11.6 us -> 10.2 us
    unnamed x34, local copies, waits for them, and re-layouts: 1.62 us -> 0.09 us
    all_to_all x1, waiting for transfers between devices: 5.14 us -> 3.66 us  [on_device(): lax.all_to_all(arrange(meta, weight), ('gx', 'gy'), 0, 0, tiled=True)]
    pallas_call x1 -> x2, Pallas kernels: 2.19 us -> 2.15 us  [the longest x1 1.43 us: choose(): pl.pallas_call(choose_kernel, out_shape=shaped(floor.shape[0], NF + 1, LN...]
  transfers between devices with their start and end apart: 15 -> 15, of which waited for: 3 -> 3; matrix products, arithmetic and copies ran while one was open for 0% -> 0% of each run, Pallas kernels for 15% -> 17%
where the time goes in v3:
time: 81.5 us; the launch traced here: 81.1 us
  starting transfers between devices  38.3 us (47%)
  Pallas kernels  31.1 us (38%)
  waiting for transfers between devices  10.2 us (13%)
  between operations  0.97 us (1%)
    ppermute x13, starting transfers between devices, shifted(): lax.ppermute(value, axis, [(i, (i + step) % count) for i in range(count)])  18.8 us
    all_to_all x1, starting transfers between devices, on_device(): lax.all_to_all(arrange(meta, weight), ('gx', 'gy'), 0, 0, tiled=True)  12.4 us
    pallas_call x1, Pallas kernels, ocean(): pl.pallas_call(ocean_kernel, out_shape=(shaped(TILE, TILE), shaped(8, TIL...  11.2 us
    all_to_all x1, starting transfers between devices, on_device(): landed = lax.all_to_all(lifted, ('gx', 'gy'), 0, 0, tiled=True)  7.18 us
    all_to_all x1, waiting for transfers between devices, on_device(): landed = lax.all_to_all(lifted, ('gx', 'gy'), 0, 0, tiled=True)  4.38 us
    pallas_call x1, Pallas kernels, lookup(): pl.pallas_call(lookup_kernel, out_shape=shaped(ocean_cell.shape[2] // LN,...  4.24 us
    pallas_call x1, Pallas kernels, predict(): pl.pallas_call(predict_kernel, out_shape=(shaped(40, EL), shaped(64, EL),...  3.78 us
    all_to_all x1, waiting for transfers between devices, on_device(): lax.all_to_all(arrange(meta, weight), ('gx', 'gy'), 0, 0, tiled=True)  3.66 us
  transfers between devices with their start and end apart: 15, of which 3 were waited for; matrix products, arithmetic and copies ran while one was open for 0% of the time, Pallas kernels for 17%

profile of v3, /device:TPU:7, one launch (start us, length us, event | category | flops | bytes accessed | tf_op | source)
XLA Modules:
  0.0 81.1 jit_solution(11209388184467693272)
XLA Ops:
  1.2 3.7 %arrange.1 = f32[64,16,128]{2,1,0:T(8,128)} custom-call(s32[8]{0:T(128)} %compare_select_fusion.5.meta, f32[1,15,4,8192]{3,2,1,0:T(4,128)} %bitcast.15), custom_call_target="tpu_custom_call" | custom-call | flops 200000000 | bytes 1048576 | tf_op jit(solution)/shard_map/arrange/pallas_call | solution.py:125
  4.9 12.4 %all-to-all-start = ((f32[64,16,128]{2,1,0:T(8,128)}), f32[64,16,128]{2,1,0:T(8,128)S(1)}, u32[]{:S(2)}, u32[]{:S(2)}) async-start(f32[64,16,128]{2,1,0:T(8,128)} %arrange.1), calls=%async_computation | async-start | bytes 1048576 | tf_op jit(solution)/shard_map/all_to_all | solution.py:551
  17.4 3.8 %predict.1 = (f32[40,1152]{1,0:T(8,128)S(1)}, f32[64,1152]{1,0:T(8,128)S(1)}, f32[16,1408]{1,0:T(8,128)S(1)}) custom-call(f32[9,35,128]{2,1,0:T(8,128)S(1)} %copy-done.5, f32[9,9,3,128]{3,2,1,0:T(4,128)S(1)} %bitcast.7, f32[3,35,35]{2,1,0:T(8,128)S(1)} %copy-done.10, f32[15,4,35]{2,1,0:T(4,128)S(1)} %bitcast.12, s32[6,16]{1,0:T(8,128)S(1)} %copy-done.13, ...), custom_call_target="tpu_custom_call" | custom-call | flops 800000000 | bytes 1048576 | tf_op jit(solution)/shard_map/predict/pallas_call | solution.py:276
  21.2 1.4 %collective-permute-start = (f32[16,1408]{1,0:T(8,128)S(1)}, f32[16,1408]{1,0:T(8,128)S(1)}, u32[]{:S(2)}, u32[]{:S(2)}) collective-permute-start(f32[16,1408]{1,0:T(8,128)S(1)} %get-tuple-element.18), channel_id=1, source_target_pairs={{0,1},{1,2},{2,3},{3,0},{4,5},{5,6},{6,7},{7,4},{8,9},{9,10},{10,1... | collective-permute-start | bytes 270344 | tf_op jit(solution)/shard_map/ppermute | solution.py:517
  22.5 1.5 %collective-permute-start.1 = (f32[16,1408]{1,0:T(8,128)S(1)}, f32[16,1408]{1,0:T(8,128)S(1)}, u32[]{:S(2)}, u32[]{:S(2)}) collective-permute-start(f32[16,1408]{1,0:T(8,128)S(1)} %get-tuple-element.18), channel_id=1, source_target_pairs={{0,3},{1,0},{2,1},{3,2},{4,7},{5,4},{6,5},{7,6},{8,11},{9,8},{10,9... | collective-permute-start | bytes 270344 | tf_op jit(solution)/shard_map/ppermute | solution.py:517
  24.1 1.4 %choose.1.chosen = f32[64,16,128]{2,1,0:T(8,128)S(1)} custom-call(f32[64,1152]{1,0:T(8,128)S(1)} %get-tuple-element.17.trace, s32[64,128]{1,0:T(8,128)S(1)} %bitcast.10), custom_call_target="tpu_custom_call" | custom-call | flops 400000000 | bytes 1048576 | tf_op jit(solution)/shard_map/choose/pallas_call | solution.py:305
  25.5 4.2 %lookup.1.heights = f32[64,128]{1,0:T(8,128)S(1)} custom-call(s32[8]{0:T(128)S(1)} %copy-done, s32[1,4,8192]{2,1,0:T(4,128)S(1)} %copy-done.9, f32[256,256]{1,0:T(8,128)S(1)} %copy-done.1), custom_call_target="tpu_custom_call" | custom-call | flops 1200000000 | bytes 1048576 | tf_op jit(solution)/shard_map/lookup/pallas_call | solution.py:170
  29.8 3.7 %all-to-all-done.inbound = f32[64,16,128]{2,1,0:T(8,128)S(1)} async-done(((f32[64,16,128]{2,1,0:T(8,128)}), f32[64,16,128]{2,1,0:T(8,128)S(1)}, u32[]{:S(2)}, u32[]{:S(2)}) %all-to-all-start) | async-done | bytes 524320 | tf_op jit(solution)/shard_map/all_to_all | solution.py:551
  33.5 0.7 uplift.1
  34.2 7.2 %all-to-all-start.1 = ((f32[64,2,128]{2,1,0:T(2,128)}), f32[64,2,128]{2,1,0:T(2,128)S(1)}, u32[]{:S(2)}, u32[]{:S(2)}) async-start(f32[64,2,128]{2,1,0:T(2,128)} %uplift.1), calls=%async_computation.1 | async-start | bytes 131072 | tf_op jit(solution)/shard_map/all_to_all | solution.py:560
  41.4 1.3 %collective-permute-start.2 = (f32[16,1408]{1,0:T(8,128)S(1)}, f32[16,1408]{1,0:T(8,128)S(1)}, u32[]{:S(2)}, u32[]{:S(2)}) collective-permute-start(f32[16,1408]{1,0:T(8,128)S(1)} %get-tuple-element.18), channel_id=1, source_target_pairs={{0,32},{32,64},{64,96},{96,128},{128,160},{160,192},{192,224},{224... | collective-permute-start | bytes 270344 | tf_op jit(solution)/shard_map/ppermute | solution.py:517
  42.6 1.6 %collective-permute-start.3 = (f32[16,1408]{1,0:T(8,128)S(1)}, f32[16,1408]{1,0:T(8,128)S(1)}, u32[]{:S(2)}, u32[]{:S(2)}) collective-permute-start(f32[16,1408]{1,0:T(8,128)S(1)} %get-tuple-element.18), channel_id=1, source_target_pairs={{0,224},{32,0},{64,32},{96,64},{128,96},{160,128},{192,160},{224,1... | collective-permute-start | bytes 270344 | tf_op jit(solution)/shard_map/ppermute | solution.py:517
  44.2 0.9 %collective-permute-start.4 = (f32[16,1408]{1,0:T(8,128)S(1)}, f32[16,1408]{1,0:T(8,128)S(1)}, u32[]{:S(2)}, u32[]{:S(2)}) collective-permute-start(f32[16,1408]{1,0:T(8,128)S(1)} %get-tuple-element.18), channel_id=1, source_target_pairs={{0,4},{4,8},{8,12},{12,16},{16,20},{20,24},{24,28},{28,0},{1,5},{5... | collective-permute-start | bytes 270344 | tf_op jit(solution)/shard_map/ppermute | solution.py:517
  45.1 4.4 %all-to-all-done.1.landed.first = f32[64,2,128]{2,1,0:T(2,128)S(1)} async-done(((f32[64,2,128]{2,1,0:T(2,128)}), f32[64,2,128]{2,1,0:T(2,128)S(1)}, u32[]{:S(2)}, u32[]{:S(2)}) %all-to-all-start.1) | async-done | bytes 65568 | tf_op jit(solution)/shard_map/all_to_all | solution.py:560
  49.5 1.3 %collective-permute-start.6 = (f32[64,2,128]{2,1,0:T(2,128)S(1)}, f32[64,2,128]{2,1,0:T(2,128)S(1)}, u32[]{:S(2)}, u32[]{:S(2)}) collective-permute-start(f32[64,2,128]{2,1,0:T(2,128)S(1)} %all-to-all-done.1.landed.first), channel_id=1, source_target_pairs={{0,1},{1,2},{2,3},{3,0},{4,5},{5,6},{6,7},{7,4},{8,9},{9,10},{10,1... | collective-permute-start | bytes 196616 | tf_op jit(solution)/shard_map/ppermute | solution.py:517
  50.8 2.6 %collective-permute-start.7 = (f32[64,2,128]{2,1,0:T(2,128)S(1)}, f32[64,2,128]{2,1,0:T(2,128)S(1)}, u32[]{:S(2)}, u32[]{:S(2)}) collective-permute-start(f32[64,2,128]{2,1,0:T(2,128)S(1)} %all-to-all-done.1.landed.first), channel_id=1, source_target_pairs={{0,2},{1,3},{2,0},{3,1},{4,6},{5,7},{6,4},{7,5},{8,10},{9,11},{10,... | collective-permute-start | bytes 196616 | tf_op jit(solution)/shard_map/ppermute | solution.py:517
  53.4 1.1 %collective-permute-start.8 = (f32[64,2,128]{2,1,0:T(2,128)S(1)}, f32[64,2,128]{2,1,0:T(2,128)S(1)}, u32[]{:S(2)}, u32[]{:S(2)}) collective-permute-start(f32[64,2,128]{2,1,0:T(2,128)S(1)} %all-to-all-done.1.landed.first), channel_id=1, source_target_pairs={{0,3},{1,0},{2,1},{3,2},{4,7},{5,4},{6,5},{7,6},{8,11},{9,8},{10,9... | collective-permute-start | bytes 196616 | tf_op jit(solution)/shard_map/ppermute | solution.py:517
  54.5 2.3 %pressure.1.load = f32[64,128]{1,0:T(8,128)S(1)} custom-call(f32[64,16,128]{2,1,0:T(8,128)S(1)} %all-to-all-done.inbound, f32[64,2,128]{2,1,0:T(2,128)S(1)} %all-to-all-done.1.landed.first, s32[64,128]{1,0:T(8,128)S(1)} %bitcast.11), custom_call_target="tpu_custom_call" | custom-call | flops 600000000 | bytes 1048576 | tf_op jit(solution)/shard_map/pressure/pallas_call | solution.py:352
  57.0 11.2 %ocean.1 = (f32[256,256]{1,0:T(8,128)}, f32[8,256]{1,0:T(8,128)S(1)}) custom-call(s32[8]{0:T(128)S(1)} %copy-done, f32[64,2,128]{2,1,0:T(2,128)S(1)} %all-to-all-done.1.landed.first, f32[64,2,128]{2,1,0:T(2,128)S(1)} %collective-permute-done.6.second, f32[64,2,128]{2,1,0:T(2,128)S(1)} %collective-permute-done.7.third, ...), custom_call_target="tpu_custom_call" | custom-call | flops 2000000000 | bytes 1048576 | tf_op jit(solution)/shard_map/ocean/pallas_call | solution.py:476
  68.5 2.4 %collective-permute-start.10 = (f32[8,256]{1,0:T(8,128)S(1)}, f32[8,256]{1,0:T(8,128)S(1)}, u32[]{:S(2)}, u32[]{:S(2)}) collective-permute-start(f32[8,256]{1,0:T(8,128)S(1)} %get-tuple-element.25), channel_id=1, source_target_pairs={{0,224},{32,0},{64,32},{96,64},{128,96},{160,128},{192,160},{224,1... | collective-permute-start | bytes 24584 | tf_op jit(solution)/shard_map/ppermute | solution.py:517
  70.8 4.4 %collective-permute-start.11 = (f32[8,256]{1,0:T(8,128)S(1)}, f32[8,256]{1,0:T(8,128)S(1)}, u32[]{:S(2)}, u32[]{:S(2)}) collective-permute-start(f32[8,256]{1,0:T(8,128)S(1)} %get-tuple-element.25), channel_id=1, source_target_pairs={{0,4},{4,8},{8,12},{12,16},{16,20},{20,24},{24,28},{28,0},{1,5},{5... | collective-permute-start | bytes 24584 | tf_op jit(solution)/shard_map/ppermute | solution.py:517
  75.3 2.2 %flux.1 = f32[9,35,128]{2,1,0:T(8,128)} custom-call(s32[8]{0:T(128)S(1)} %copy-done, f32[9,35,128]{2,1,0:T(8,128)S(1)} %copy-done.5, f32[40,1152]{1,0:T(8,128)S(1)} %get-tuple-element.16.base, f32[64,128]{1,0:T(8,128)S(1)} %pressure.1.load, f32[64,1152]{1,0:T(8,128)S(1)} %get-tuple-element.17.trace, f32[16,1408]{1,0:T(8,128)S(1)} %collective-permute-done.2.below_x, ...), custom_call_target="tpu_custom_call" | custom-call | flops 800000000 | bytes 1048576 | tf_op jit(solution)/shard_map/flux/pallas_call | solution.py:410
  77.5 2.1 %collective-permute-done.12.above_y = f32[8,256]{1,0:T(8,128)S(1)} collective-permute-done((f32[8,256]{1,0:T(8,128)S(1)}, f32[8,256]{1,0:T(8,128)S(1)}, u32[]{:S(2)}, u32[]{:S(2)}) %collective-permute-start.12) | collective-permute-done | bytes 8224 | tf_op jit(solution)/shard_map/ppermute | solution.py:517
  79.6 1.6 %flow.1 = (f32[256,256]{1,0:T(8,128)}, f32[256,256]{1,0:T(8,128)}) custom-call(s32[8]{0:T(128)S(1)} %copy-done, f32[256,256]{1,0:T(8,128)S(1)} %copy-done.16, f32[256,256]{1,0:T(8,128)S(1)} %copy-done.3, f32[256,256]{1,0:T(8,128)S(1)} %copy-done.4, f32[8,256]{1,0:T(8,128)S(1)} %collective-permute-done.9.below_x, ...), custom_call_target="tpu_custom_call" | custom-call | flops 400000000 | bytes 1048576 | tf_op jit(solution)/shard_map/flow/pallas_call | solution.py:504
  (50 shorter events, 1.0 us)
Async XLA Ops:
  0.6 16.6 %copy-start.5 = (f32[9,35,128]{2,1,0:T(8,128)S(1)}, f32[9,35,128]{2,1,0:T(8,128)}, u32[]{:S(2)}) copy-start(f32[9,35,128]{2,1,0:T(8,128)} %state.3) | copy-start | bytes 483844
  0.6 16.6 %copy-start.6 = (f32[3,9,9,128]{3,0,2,1:T(4,128)S(1)}, f32[3,9,9,128]{3,0,2,1:T(4,128)}, u32[]{:S(2)}) copy-start(f32[3,9,9,128]{3,0,2,1:T(4,128)} %param.17) | copy-start | bytes 373252
  0.7 16.6 %copy-start.10 = (f32[3,35,35]{2,1,0:T(8,128)S(1)}, f32[3,35,35]{2,1,0:T(8,128)}, u32[]{:S(2)}) copy-start(f32[3,35,35]{2,1,0:T(8,128)} %stiffness.1) | copy-start | bytes 44104
  4.9 19.2 %copy-start.11 = (s32[8192]{0:T(1024)S(1)}, s32[8192]{0:T(1024)}, u32[]{:S(2)}) copy-start(s32[8192]{0:T(1024)} %param.25) | copy-start | bytes 98308
  4.9 28.6 %all-to-all-start = ((f32[64,16,128]{2,1,0:T(8,128)}), f32[64,16,128]{2,1,0:T(8,128)S(1)}, u32[]{:S(2)}, u32[]{:S(2)}) async-start(f32[64,16,128]{2,1,0:T(8,128)} %arrange.1), calls=%async_computation | async-start | bytes 1048576 | tf_op jit(solution)/shard_map/all_to_all | solution.py:551
  21.2 8.6 %collective-permute-start = (f32[16,1408]{1,0:T(8,128)S(1)}, f32[16,1408]{1,0:T(8,128)S(1)}, u32[]{:S(2)}, u32[]{:S(2)}) collective-permute-start(f32[16,1408]{1,0:T(8,128)S(1)} %get-tuple-element.18), channel_id=1, source_target_pairs={{0,1},{1,2},{2,3},{3,0},{4,5},{5,6},{6,7},{7,4},{8,9},{9,10},{10,1... | collective-permute-start | bytes 270344 | tf_op jit(solution)/shard_map/ppermute | solution.py:517
  22.5 7.3 %collective-permute-start.1 = (f32[16,1408]{1,0:T(8,128)S(1)}, f32[16,1408]{1,0:T(8,128)S(1)}, u32[]{:S(2)}, u32[]{:S(2)}) collective-permute-start(f32[16,1408]{1,0:T(8,128)S(1)} %get-tuple-element.18), channel_id=1, source_target_pairs={{0,3},{1,0},{2,1},{3,2},{4,7},{5,4},{6,5},{7,6},{8,11},{9,8},{10,9... | collective-permute-start | bytes 270344 | tf_op jit(solution)/shard_map/ppermute | solution.py:517
  29.8 27.2 %copy-start.2 = (f32[256,256]{1,0:T(8,128)S(1)}, f32[256,256]{1,0:T(8,128)}, u32[]{:S(2)}) copy-start(f32[256,256]{1,0:T(8,128)} %depth.1) | copy-start | bytes 786436
  34.2 15.3 %all-to-all-start.1 = ((f32[64,2,128]{2,1,0:T(2,128)}), f32[64,2,128]{2,1,0:T(2,128)S(1)}, u32[]{:S(2)}, u32[]{:S(2)}) async-start(f32[64,2,128]{2,1,0:T(2,128)} %uplift.1), calls=%async_computation.1 | async-start | bytes 131072 | tf_op jit(solution)/shard_map/all_to_all | solution.py:560
  41.4 9.5 %collective-permute-start.2 = (f32[16,1408]{1,0:T(8,128)S(1)}, f32[16,1408]{1,0:T(8,128)S(1)}, u32[]{:S(2)}, u32[]{:S(2)}) collective-permute-start(f32[16,1408]{1,0:T(8,128)S(1)} %get-tuple-element.18), channel_id=1, source_target_pairs={{0,32},{32,64},{64,96},{96,128},{128,160},{160,192},{192,224},{224... | collective-permute-start | bytes 270344 | tf_op jit(solution)/shard_map/ppermute | solution.py:517
  42.6 10.8 %collective-permute-start.3 = (f32[16,1408]{1,0:T(8,128)S(1)}, f32[16,1408]{1,0:T(8,128)S(1)}, u32[]{:S(2)}, u32[]{:S(2)}) collective-permute-start(f32[16,1408]{1,0:T(8,128)S(1)} %get-tuple-element.18), channel_id=1, source_target_pairs={{0,224},{32,0},{64,32},{96,64},{128,96},{160,128},{192,160},{224,1... | collective-permute-start | bytes 270344 | tf_op jit(solution)/shard_map/ppermute | solution.py:517
  44.2 12.7 %collective-permute-start.4 = (f32[16,1408]{1,0:T(8,128)S(1)}, f32[16,1408]{1,0:T(8,128)S(1)}, u32[]{:S(2)}, u32[]{:S(2)}) collective-permute-start(f32[16,1408]{1,0:T(8,128)S(1)} %get-tuple-element.18), channel_id=1, source_target_pairs={{0,4},{4,8},{8,12},{12,16},{16,20},{20,24},{24,28},{28,0},{1,5},{5... | collective-permute-start | bytes 270344 | tf_op jit(solution)/shard_map/ppermute | solution.py:517
  45.1 11.8 %collective-permute-start.5 = (f32[16,1408]{1,0:T(8,128)S(1)}, f32[16,1408]{1,0:T(8,128)S(1)}, u32[]{:S(2)}, u32[]{:S(2)}) collective-permute-start(f32[16,1408]{1,0:T(8,128)S(1)} %get-tuple-element.18), channel_id=1, source_target_pairs={{0,28},{4,0},{8,4},{12,8},{16,12},{20,16},{24,20},{28,24},{1,29},{... | collective-permute-start | bytes 270344 | tf_op jit(solution)/shard_map/ppermute | solution.py:517
  49.5 7.4 %collective-permute-start.6 = (f32[64,2,128]{2,1,0:T(2,128)S(1)}, f32[64,2,128]{2,1,0:T(2,128)S(1)}, u32[]{:S(2)}, u32[]{:S(2)}) collective-permute-start(f32[64,2,128]{2,1,0:T(2,128)S(1)} %all-to-all-done.1.landed.first), channel_id=1, source_target_pairs={{0,1},{1,2},{2,3},{3,0},{4,5},{5,6},{6,7},{7,4},{8,9},{9,10},{10,1... | collective-permute-start | bytes 196616 | tf_op jit(solution)/shard_map/ppermute | solution.py:517
  50.8 6.1 %collective-permute-start.7 = (f32[64,2,128]{2,1,0:T(2,128)S(1)}, f32[64,2,128]{2,1,0:T(2,128)S(1)}, u32[]{:S(2)}, u32[]{:S(2)}) collective-permute-start(f32[64,2,128]{2,1,0:T(2,128)S(1)} %all-to-all-done.1.landed.first), channel_id=1, source_target_pairs={{0,2},{1,3},{2,0},{3,1},{4,6},{5,7},{6,4},{7,5},{8,10},{9,11},{10,... | collective-permute-start | bytes 196616 | tf_op jit(solution)/shard_map/ppermute | solution.py:517
  53.4 3.5 %collective-permute-start.8 = (f32[64,2,128]{2,1,0:T(2,128)S(1)}, f32[64,2,128]{2,1,0:T(2,128)S(1)}, u32[]{:S(2)}, u32[]{:S(2)}) collective-permute-start(f32[64,2,128]{2,1,0:T(2,128)S(1)} %all-to-all-done.1.landed.first), channel_id=1, source_target_pairs={{0,3},{1,0},{2,1},{3,2},{4,7},{5,4},{6,5},{7,6},{8,11},{9,8},{10,9... | collective-permute-start | bytes 196616 | tf_op jit(solution)/shard_map/ppermute | solution.py:517
  56.9 18.4 %copy-start.7 = (f32[4,9,9,128]{3,0,2,1:T(4,128)S(1)}, f32[4,9,9,128]{3,0,2,1:T(4,128)}, u32[]{:S(2)}) copy-start(f32[4,9,9,128]{3,0,2,1:T(4,128)} %param.20) | copy-start | bytes 497668
  56.9 18.4 %copy-start.8 = (f32[4,9,9,128]{3,0,2,1:T(4,128)S(1)}, f32[4,9,9,128]{3,0,2,1:T(4,128)}, u32[]{:S(2)}) copy-start(f32[4,9,9,128]{3,0,2,1:T(4,128)} %param.21) | copy-start | bytes 497668
  56.9 18.4 %copy-start.14 = (s32[4,128]{1,0:T(4,128)S(1)}, s32[4,128]{1,0:T(4,128)}, u32[]{:S(2)}) copy-start(s32[4,128]{1,0:T(4,128)} %source.1) | copy-start | bytes 6148
  56.9 18.4 %copy-start.15 = (s32[128]{0:T(128)S(1)}, s32[128]{0:T(128)}, u32[]{:S(2)}) copy-start(s32[128]{0:T(128)} %param.24) | copy-start | bytes 1540
  68.2 9.3 %collective-permute-start.9 = (f32[8,256]{1,0:T(8,128)S(1)}, f32[8,256]{1,0:T(8,128)S(1)}, u32[]{:S(2)}, u32[]{:S(2)}) collective-permute-start(f32[8,256]{1,0:T(8,128)S(1)} %get-tuple-element.25), channel_id=1, source_target_pairs={{0,32},{32,64},{64,96},{96,128},{128,160},{160,192},{192,224},{224... | collective-permute-start | bytes 24584 | tf_op jit(solution)/shard_map/ppermute | solution.py:517
  68.5 9.0 %collective-permute-start.10 = (f32[8,256]{1,0:T(8,128)S(1)}, f32[8,256]{1,0:T(8,128)S(1)}, u32[]{:S(2)}, u32[]{:S(2)}) collective-permute-start(f32[8,256]{1,0:T(8,128)S(1)} %get-tuple-element.25), channel_id=1, source_target_pairs={{0,224},{32,0},{64,32},{96,64},{128,96},{160,128},{192,160},{224,1... | collective-permute-start | bytes 24584 | tf_op jit(solution)/shard_map/ppermute | solution.py:517
  70.8 6.6 %collective-permute-start.11 = (f32[8,256]{1,0:T(8,128)S(1)}, f32[8,256]{1,0:T(8,128)S(1)}, u32[]{:S(2)}, u32[]{:S(2)}) collective-permute-start(f32[8,256]{1,0:T(8,128)S(1)} %get-tuple-element.25), channel_id=1, source_target_pairs={{0,4},{4,8},{8,12},{12,16},{16,20},{20,24},{24,28},{28,0},{1,5},{5... | collective-permute-start | bytes 24584 | tf_op jit(solution)/shard_map/ppermute | solution.py:517
  75.3 4.3 %collective-permute-start.12 = (f32[8,256]{1,0:T(8,128)S(1)}, f32[8,256]{1,0:T(8,128)S(1)}, u32[]{:S(2)}, u32[]{:S(2)}) collective-permute-start(f32[8,256]{1,0:T(8,128)S(1)} %get-tuple-element.25), channel_id=1, source_target_pairs={{0,28},{4,0},{8,4},{12,8},{16,12},{20,16},{24,20},{28,24},{1,29},{... | collective-permute-start | bytes 24584 | tf_op jit(solution)/shard_map/ppermute | solution.py:517
  (8 other events, 102.4 us)

commit v4 on v3

--- a/solution.py
+++ b/solution.py
@@ -344,7 +344,7 @@
                 left[i, 64 + f * 16 : 64 + (f + 1) * 16] = jnp.where(hit, low, zero)
         return total + joined(left, right)
 
-    total = lax.fori_loop(0, floor.shape[0] // 8, chunk, jnp.zeros((LN, LN), f32))
+    total = lax.fori_loop(0, floor.shape[0] // 8, chunk, jnp.zeros((LN, LN), f32), unroll=4)
     load[...] = total[:64] + total[64:]
 
 

time: 81.5 us -> 81.5 us (level)
  transfers between devices with their start and end apart: 15 -> 15, of which waited for: 3 -> 5; matrix products, arithmetic and copies ran while one was open for 0% -> 0% of each run, Pallas kernels for 17% -> 16%
where the time goes in v4:
time: 81.5 us; the launch traced here: 81.1 us
  starting transfers between devices  38.4 us (47%)
  Pallas kernels  30.3 us (37%)
  waiting for transfers between devices  10.8 us (13%)
  between operations  0.95 us (1%)
    ppermute x13, starting transfers between devices, shifted(): lax.ppermute(value, axis, [(i, (i + step) % count) for i in range(count)])  18.9 us
    all_to_all x1, starting transfers between devices, on_device(): lax.all_to_all(arrange(meta, weight), ('gx', 'gy'), 0, 0, tiled=True)  12.4 us
    pallas_call x1, Pallas kernels, ocean(): pl.pallas_call(ocean_kernel, out_shape=(shaped(TILE, TILE), shaped(8, TIL...  11.2 us
    all_to_all x1, starting transfers between devices, on_device(): landed = lax.all_to_all(lifted, ('gx', 'gy'), 0, 0, tiled=True)  7.18 us
    all_to_all x1, waiting for transfers between devices, on_device(): landed = lax.all_to_all(lifted, ('gx', 'gy'), 0, 0, tiled=True)  4.38 us
    pallas_call x1, Pallas kernels, lookup(): pl.pallas_call(lookup_kernel, out_shape=shaped(ocean_cell.shape[2] // LN,...  4.24 us
    pallas_call x1, Pallas kernels, predict(): pl.pallas_call(predict_kernel, out_shape=(shaped(40, EL), shaped(64, EL),...  3.78 us
    all_to_all x1, waiting for transfers between devices, on_device(): lax.all_to_all(arrange(meta, weight), ('gx', 'gy'), 0, 0, tiled=True)  3.66 us
  transfers between devices with their start and end apart: 15, of which 5 were waited for; matrix products, arithmetic and copies ran while one was open for 0% of the time, Pallas kernels for 16%

profile of v4, /device:TPU:7, one launch (start us, length us, event | category | flops | bytes accessed | tf_op | source)
XLA Modules:
  0.0 81.1 jit_solution(9297606447465479068)
XLA Ops:
  1.2 3.7 %arrange.1 = f32[64,16,128]{2,1,0:T(8,128)} custom-call(s32[8]{0:T(128)} %compare_select_fusion.5.meta, f32[1,15,4,8192]{3,2,1,0:T(4,128)} %bitcast.15), custom_call_target="tpu_custom_call" | custom-call | flops 200000000 | bytes 1048576 | tf_op jit(solution)/shard_map/arrange/pallas_call | solution.py:125
  4.9 12.4 %all-to-all-start = ((f32[64,16,128]{2,1,0:T(8,128)}), f32[64,16,128]{2,1,0:T(8,128)S(1)}, u32[]{:S(2)}, u32[]{:S(2)}) async-start(f32[64,16,128]{2,1,0:T(8,128)} %arrange.1), calls=%async_computation | async-start | bytes 1048576 | tf_op jit(solution)/shard_map/all_to_all | solution.py:551
  17.4 3.8 %predict.1 = (f32[40,1152]{1,0:T(8,128)S(1)}, f32[64,1152]{1,0:T(8,128)S(1)}, f32[16,1408]{1,0:T(8,128)S(1)}) custom-call(f32[9,35,128]{2,1,0:T(8,128)S(1)} %copy-done.5, f32[9,9,3,128]{3,2,1,0:T(4,128)S(1)} %bitcast.7, f32[3,35,35]{2,1,0:T(8,128)S(1)} %copy-done.10, f32[15,4,35]{2,1,0:T(4,128)S(1)} %bitcast.12, s32[6,16]{1,0:T(8,128)S(1)} %copy-done.13, ...), custom_call_target="tpu_custom_call" | custom-call | flops 800000000 | bytes 1048576 | tf_op jit(solution)/shard_map/predict/pallas_call | solution.py:276
  21.2 1.4 %collective-permute-start = (f32[16,1408]{1,0:T(8,128)S(1)}, f32[16,1408]{1,0:T(8,128)S(1)}, u32[]{:S(2)}, u32[]{:S(2)}) collective-permute-start(f32[16,1408]{1,0:T(8,128)S(1)} %get-tuple-element.18), channel_id=1, source_target_pairs={{0,1},{1,2},{2,3},{3,0},{4,5},{5,6},{6,7},{7,4},{8,9},{9,10},{10,1... | collective-permute-start | bytes 270344 | tf_op jit(solution)/shard_map/ppermute | solution.py:517
  22.5 1.5 %collective-permute-start.1 = (f32[16,1408]{1,0:T(8,128)S(1)}, f32[16,1408]{1,0:T(8,128)S(1)}, u32[]{:S(2)}, u32[]{:S(2)}) collective-permute-start(f32[16,1408]{1,0:T(8,128)S(1)} %get-tuple-element.18), channel_id=1, source_target_pairs={{0,3},{1,0},{2,1},{3,2},{4,7},{5,4},{6,5},{7,6},{8,11},{9,8},{10,9... | collective-permute-start | bytes 270344 | tf_op jit(solution)/shard_map/ppermute | solution.py:517
  24.1 1.4 %choose.1.chosen = f32[64,16,128]{2,1,0:T(8,128)S(1)} custom-call(f32[64,1152]{1,0:T(8,128)S(1)} %get-tuple-element.17.trace, s32[64,128]{1,0:T(8,128)S(1)} %bitcast.10), custom_call_target="tpu_custom_call" | custom-call | flops 400000000 | bytes 1048576 | tf_op jit(solution)/shard_map/choose/pallas_call | solution.py:305
  25.5 4.2 %lookup.1.heights = f32[64,128]{1,0:T(8,128)S(1)} custom-call(s32[8]{0:T(128)S(1)} %copy-done, s32[1,4,8192]{2,1,0:T(4,128)S(1)} %copy-done.9, f32[256,256]{1,0:T(8,128)S(1)} %copy-done.1), custom_call_target="tpu_custom_call" | custom-call | flops 1200000000 | bytes 1048576 | tf_op jit(solution)/shard_map/lookup/pallas_call | solution.py:170
  29.8 3.7 %all-to-all-done.inbound = f32[64,16,128]{2,1,0:T(8,128)S(1)} async-done(((f32[64,16,128]{2,1,0:T(8,128)}), f32[64,16,128]{2,1,0:T(8,128)S(1)}, u32[]{:S(2)}, u32[]{:S(2)}) %all-to-all-start) | async-done | bytes 524320 | tf_op jit(solution)/shard_map/all_to_all | solution.py:551
  33.5 0.7 uplift.1
  34.2 7.2 %all-to-all-start.1 = ((f32[64,2,128]{2,1,0:T(2,128)}), f32[64,2,128]{2,1,0:T(2,128)S(1)}, u32[]{:S(2)}, u32[]{:S(2)}) async-start(f32[64,2,128]{2,1,0:T(2,128)} %uplift.1), calls=%async_computation.1 | async-start | bytes 131072 | tf_op jit(solution)/shard_map/all_to_all | solution.py:560
  41.4 1.3 %collective-permute-start.2 = (f32[16,1408]{1,0:T(8,128)S(1)}, f32[16,1408]{1,0:T(8,128)S(1)}, u32[]{:S(2)}, u32[]{:S(2)}) collective-permute-start(f32[16,1408]{1,0:T(8,128)S(1)} %get-tuple-element.18), channel_id=1, source_target_pairs={{0,32},{32,64},{64,96},{96,128},{128,160},{160,192},{192,224},{224... | collective-permute-start | bytes 270344 | tf_op jit(solution)/shard_map/ppermute | solution.py:517
  42.6 1.6 %collective-permute-start.3 = (f32[16,1408]{1,0:T(8,128)S(1)}, f32[16,1408]{1,0:T(8,128)S(1)}, u32[]{:S(2)}, u32[]{:S(2)}) collective-permute-start(f32[16,1408]{1,0:T(8,128)S(1)} %get-tuple-element.18), channel_id=1, source_target_pairs={{0,224},{32,0},{64,32},{96,64},{128,96},{160,128},{192,160},{224,1... | collective-permute-start | bytes 270344 | tf_op jit(solution)/shard_map/ppermute | solution.py:517
  44.2 0.9 %collective-permute-start.4 = (f32[16,1408]{1,0:T(8,128)S(1)}, f32[16,1408]{1,0:T(8,128)S(1)}, u32[]{:S(2)}, u32[]{:S(2)}) collective-permute-start(f32[16,1408]{1,0:T(8,128)S(1)} %get-tuple-element.18), channel_id=1, source_target_pairs={{0,4},{4,8},{8,12},{12,16},{16,20},{20,24},{24,28},{28,0},{1,5},{5... | collective-permute-start | bytes 270344 | tf_op jit(solution)/shard_map/ppermute | solution.py:517
  45.1 4.4 %all-to-all-done.1.landed.first = f32[64,2,128]{2,1,0:T(2,128)S(1)} async-done(((f32[64,2,128]{2,1,0:T(2,128)}), f32[64,2,128]{2,1,0:T(2,128)S(1)}, u32[]{:S(2)}, u32[]{:S(2)}) %all-to-all-start.1) | async-done | bytes 65568 | tf_op jit(solution)/shard_map/all_to_all | solution.py:560
  49.5 1.3 %collective-permute-start.6 = (f32[64,2,128]{2,1,0:T(2,128)S(1)}, f32[64,2,128]{2,1,0:T(2,128)S(1)}, u32[]{:S(2)}, u32[]{:S(2)}) collective-permute-start(f32[64,2,128]{2,1,0:T(2,128)S(1)} %all-to-all-done.1.landed.first), channel_id=1, source_target_pairs={{0,1},{1,2},{2,3},{3,0},{4,5},{5,6},{6,7},{7,4},{8,9},{9,10},{10,1... | collective-permute-start | bytes 196616 | tf_op jit(solution)/shard_map/ppermute | solution.py:517
  50.8 2.6 %collective-permute-start.7 = (f32[64,2,128]{2,1,0:T(2,128)S(1)}, f32[64,2,128]{2,1,0:T(2,128)S(1)}, u32[]{:S(2)}, u32[]{:S(2)}) collective-permute-start(f32[64,2,128]{2,1,0:T(2,128)S(1)} %all-to-all-done.1.landed.first), channel_id=1, source_target_pairs={{0,2},{1,3},{2,0},{3,1},{4,6},{5,7},{6,4},{7,5},{8,10},{9,11},{10,... | collective-permute-start | bytes 196616 | tf_op jit(solution)/shard_map/ppermute | solution.py:517
  53.4 1.1 %collective-permute-start.8 = (f32[64,2,128]{2,1,0:T(2,128)S(1)}, f32[64,2,128]{2,1,0:T(2,128)S(1)}, u32[]{:S(2)}, u32[]{:S(2)}) collective-permute-start(f32[64,2,128]{2,1,0:T(2,128)S(1)} %all-to-all-done.1.landed.first), channel_id=1, source_target_pairs={{0,3},{1,0},{2,1},{3,2},{4,7},{5,4},{6,5},{7,6},{8,11},{9,8},{10,9... | collective-permute-start | bytes 196616 | tf_op jit(solution)/shard_map/ppermute | solution.py:517
  54.5 1.6 %pressure.1.load = f32[64,128]{1,0:T(8,128)S(1)} custom-call(f32[64,16,128]{2,1,0:T(8,128)S(1)} %all-to-all-done.inbound, f32[64,2,128]{2,1,0:T(2,128)S(1)} %all-to-all-done.1.landed.first, s32[64,128]{1,0:T(8,128)S(1)} %bitcast.11), custom_call_target="tpu_custom_call" | custom-call | flops 600000000 | bytes 1048576 | tf_op jit(solution)/shard_map/pressure/pallas_call | solution.py:352
  56.9 11.2 %ocean.1 = (f32[256,256]{1,0:T(8,128)}, f32[8,256]{1,0:T(8,128)S(1)}) custom-call(s32[8]{0:T(128)S(1)} %copy-done, f32[64,2,128]{2,1,0:T(2,128)S(1)} %all-to-all-done.1.landed.first, f32[64,2,128]{2,1,0:T(2,128)S(1)} %collective-permute-done.6.second, f32[64,2,128]{2,1,0:T(2,128)S(1)} %collective-permute-done.7.third, ...), custom_call_target="tpu_custom_call" | custom-call | flops 2000000000 | bytes 1048576 | tf_op jit(solution)/shard_map/ocean/pallas_call | solution.py:476
  68.4 2.3 %collective-permute-start.10 = (f32[8,256]{1,0:T(8,128)S(1)}, f32[8,256]{1,0:T(8,128)S(1)}, u32[]{:S(2)}, u32[]{:S(2)}) collective-permute-start(f32[8,256]{1,0:T(8,128)S(1)} %get-tuple-element.25), channel_id=1, source_target_pairs={{0,224},{32,0},{64,32},{96,64},{128,96},{160,128},{192,160},{224,1... | collective-permute-start | bytes 24584 | tf_op jit(solution)/shard_map/ppermute | solution.py:517
  70.7 4.5 %collective-permute-start.11 = (f32[8,256]{1,0:T(8,128)S(1)}, f32[8,256]{1,0:T(8,128)S(1)}, u32[]{:S(2)}, u32[]{:S(2)}) collective-permute-start(f32[8,256]{1,0:T(8,128)S(1)} %get-tuple-element.25), channel_id=1, source_target_pairs={{0,4},{4,8},{8,12},{12,16},{16,20},{20,24},{24,28},{28,0},{1,5},{5... | collective-permute-start | bytes 24584 | tf_op jit(solution)/shard_map/ppermute | solution.py:517
  75.3 2.2 %flux.1 = f32[9,35,128]{2,1,0:T(8,128)} custom-call(s32[8]{0:T(128)S(1)} %copy-done, f32[9,35,128]{2,1,0:T(8,128)S(1)} %copy-done.5, f32[40,1152]{1,0:T(8,128)S(1)} %get-tuple-element.16.base, f32[64,128]{1,0:T(8,128)S(1)} %pressure.1.load, f32[64,1152]{1,0:T(8,128)S(1)} %get-tuple-element.17.trace, f32[16,1408]{1,0:T(8,128)S(1)} %collective-permute-done.2.below_x, ...), custom_call_target="tpu_custom_call" | custom-call | flops 800000000 | bytes 1048576 | tf_op jit(solution)/shard_map/flux/pallas_call | solution.py:410
  77.5 2.1 %collective-permute-done.12.above_y = f32[8,256]{1,0:T(8,128)S(1)} collective-permute-done((f32[8,256]{1,0:T(8,128)S(1)}, f32[8,256]{1,0:T(8,128)S(1)}, u32[]{:S(2)}, u32[]{:S(2)}) %collective-permute-start.12) | collective-permute-done | bytes 8224 | tf_op jit(solution)/shard_map/ppermute | solution.py:517
  79.6 1.6 %flow.1 = (f32[256,256]{1,0:T(8,128)}, f32[256,256]{1,0:T(8,128)}) custom-call(s32[8]{0:T(128)S(1)} %copy-done, f32[256,256]{1,0:T(8,128)S(1)} %copy-done.16, f32[256,256]{1,0:T(8,128)S(1)} %copy-done.3, f32[256,256]{1,0:T(8,128)S(1)} %copy-done.4, f32[8,256]{1,0:T(8,128)S(1)} %collective-permute-done.9.below_x, ...), custom_call_target="tpu_custom_call" | custom-call | flops 400000000 | bytes 1048576 | tf_op jit(solution)/shard_map/flow/pallas_call | solution.py:504
  (50 shorter events, 1.6 us)
Async XLA Ops:
  0.6 16.6 %copy-start.5 = (f32[9,35,128]{2,1,0:T(8,128)S(1)}, f32[9,35,128]{2,1,0:T(8,128)}, u32[]{:S(2)}) copy-start(f32[9,35,128]{2,1,0:T(8,128)} %state.3) | copy-start | bytes 483844
  0.6 16.6 %copy-start.6 = (f32[3,9,9,128]{3,0,2,1:T(4,128)S(1)}, f32[3,9,9,128]{3,0,2,1:T(4,128)}, u32[]{:S(2)}) copy-start(f32[3,9,9,128]{3,0,2,1:T(4,128)} %param.17) | copy-start | bytes 373252
  0.7 16.6 %copy-start.10 = (f32[3,35,35]{2,1,0:T(8,128)S(1)}, f32[3,35,35]{2,1,0:T(8,128)}, u32[]{:S(2)}) copy-start(f32[3,35,35]{2,1,0:T(8,128)} %stiffness.1) | copy-start | bytes 44104
  4.9 19.2 %copy-start.11 = (s32[8192]{0:T(1024)S(1)}, s32[8192]{0:T(1024)}, u32[]{:S(2)}) copy-start(s32[8192]{0:T(1024)} %param.25) | copy-start | bytes 98308
  4.9 28.6 %all-to-all-start = ((f32[64,16,128]{2,1,0:T(8,128)}), f32[64,16,128]{2,1,0:T(8,128)S(1)}, u32[]{:S(2)}, u32[]{:S(2)}) async-start(f32[64,16,128]{2,1,0:T(8,128)} %arrange.1), calls=%async_computation | async-start | bytes 1048576 | tf_op jit(solution)/shard_map/all_to_all | solution.py:551
  21.2 8.6 %collective-permute-start = (f32[16,1408]{1,0:T(8,128)S(1)}, f32[16,1408]{1,0:T(8,128)S(1)}, u32[]{:S(2)}, u32[]{:S(2)}) collective-permute-start(f32[16,1408]{1,0:T(8,128)S(1)} %get-tuple-element.18), channel_id=1, source_target_pairs={{0,1},{1,2},{2,3},{3,0},{4,5},{5,6},{6,7},{7,4},{8,9},{9,10},{10,1... | collective-permute-start | bytes 270344 | tf_op jit(solution)/shard_map/ppermute | solution.py:517
  22.5 7.3 %collective-permute-start.1 = (f32[16,1408]{1,0:T(8,128)S(1)}, f32[16,1408]{1,0:T(8,128)S(1)}, u32[]{:S(2)}, u32[]{:S(2)}) collective-permute-start(f32[16,1408]{1,0:T(8,128)S(1)} %get-tuple-element.18), channel_id=1, source_target_pairs={{0,3},{1,0},{2,1},{3,2},{4,7},{5,4},{6,5},{7,6},{8,11},{9,8},{10,9... | collective-permute-start | bytes 270344 | tf_op jit(solution)/shard_map/ppermute | solution.py:517
  29.8 27.1 %copy-start.2 = (f32[256,256]{1,0:T(8,128)S(1)}, f32[256,256]{1,0:T(8,128)}, u32[]{:S(2)}) copy-start(f32[256,256]{1,0:T(8,128)} %depth.1) | copy-start | bytes 786436
  34.2 15.3 %all-to-all-start.1 = ((f32[64,2,128]{2,1,0:T(2,128)}), f32[64,2,128]{2,1,0:T(2,128)S(1)}, u32[]{:S(2)}, u32[]{:S(2)}) async-start(f32[64,2,128]{2,1,0:T(2,128)} %uplift.1), calls=%async_computation.1 | async-start | bytes 131072 | tf_op jit(solution)/shard_map/all_to_all | solution.py:560
  41.4 9.5 %collective-permute-start.2 = (f32[16,1408]{1,0:T(8,128)S(1)}, f32[16,1408]{1,0:T(8,128)S(1)}, u32[]{:S(2)}, u32[]{:S(2)}) collective-permute-start(f32[16,1408]{1,0:T(8,128)S(1)} %get-tuple-element.18), channel_id=1, source_target_pairs={{0,32},{32,64},{64,96},{96,128},{128,160},{160,192},{192,224},{224... | collective-permute-start | bytes 270344 | tf_op jit(solution)/shard_map/ppermute | solution.py:517
  42.6 10.8 %collective-permute-start.3 = (f32[16,1408]{1,0:T(8,128)S(1)}, f32[16,1408]{1,0:T(8,128)S(1)}, u32[]{:S(2)}, u32[]{:S(2)}) collective-permute-start(f32[16,1408]{1,0:T(8,128)S(1)} %get-tuple-element.18), channel_id=1, source_target_pairs={{0,224},{32,0},{64,32},{96,64},{128,96},{160,128},{192,160},{224,1... | collective-permute-start | bytes 270344 | tf_op jit(solution)/shard_map/ppermute | solution.py:517
  44.2 11.9 %collective-permute-start.4 = (f32[16,1408]{1,0:T(8,128)S(1)}, f32[16,1408]{1,0:T(8,128)S(1)}, u32[]{:S(2)}, u32[]{:S(2)}) collective-permute-start(f32[16,1408]{1,0:T(8,128)S(1)} %get-tuple-element.18), channel_id=1, source_target_pairs={{0,4},{4,8},{8,12},{12,16},{16,20},{20,24},{24,28},{28,0},{1,5},{5... | collective-permute-start | bytes 270344 | tf_op jit(solution)/shard_map/ppermute | solution.py:517
  45.1 11.0 %collective-permute-start.5 = (f32[16,1408]{1,0:T(8,128)S(1)}, f32[16,1408]{1,0:T(8,128)S(1)}, u32[]{:S(2)}, u32[]{:S(2)}) collective-permute-start(f32[16,1408]{1,0:T(8,128)S(1)} %get-tuple-element.18), channel_id=1, source_target_pairs={{0,28},{4,0},{8,4},{12,8},{16,12},{20,16},{24,20},{28,24},{1,29},{... | collective-permute-start | bytes 270344 | tf_op jit(solution)/shard_map/ppermute | solution.py:517
  49.5 6.7 %collective-permute-start.6 = (f32[64,2,128]{2,1,0:T(2,128)S(1)}, f32[64,2,128]{2,1,0:T(2,128)S(1)}, u32[]{:S(2)}, u32[]{:S(2)}) collective-permute-start(f32[64,2,128]{2,1,0:T(2,128)S(1)} %all-to-all-done.1.landed.first), channel_id=1, source_target_pairs={{0,1},{1,2},{2,3},{3,0},{4,5},{5,6},{6,7},{7,4},{8,9},{9,10},{10,1... | collective-permute-start | bytes 196616 | tf_op jit(solution)/shard_map/ppermute | solution.py:517
  50.8 5.5 %collective-permute-start.7 = (f32[64,2,128]{2,1,0:T(2,128)S(1)}, f32[64,2,128]{2,1,0:T(2,128)S(1)}, u32[]{:S(2)}, u32[]{:S(2)}) collective-permute-start(f32[64,2,128]{2,1,0:T(2,128)S(1)} %all-to-all-done.1.landed.first), channel_id=1, source_target_pairs={{0,2},{1,3},{2,0},{3,1},{4,6},{5,7},{6,4},{7,5},{8,10},{9,11},{10,... | collective-permute-start | bytes 196616 | tf_op jit(solution)/shard_map/ppermute | solution.py:517
  53.4 3.4 %collective-permute-start.8 = (f32[64,2,128]{2,1,0:T(2,128)S(1)}, f32[64,2,128]{2,1,0:T(2,128)S(1)}, u32[]{:S(2)}, u32[]{:S(2)}) collective-permute-start(f32[64,2,128]{2,1,0:T(2,128)S(1)} %all-to-all-done.1.landed.first), channel_id=1, source_target_pairs={{0,3},{1,0},{2,1},{3,2},{4,7},{5,4},{6,5},{7,6},{8,11},{9,8},{10,9... | collective-permute-start | bytes 196616 | tf_op jit(solution)/shard_map/ppermute | solution.py:517
  56.1 19.2 %copy-start.7 = (f32[4,9,9,128]{3,0,2,1:T(4,128)S(1)}, f32[4,9,9,128]{3,0,2,1:T(4,128)}, u32[]{:S(2)}) copy-start(f32[4,9,9,128]{3,0,2,1:T(4,128)} %param.20) | copy-start | bytes 497668
  56.1 19.2 %copy-start.8 = (f32[4,9,9,128]{3,0,2,1:T(4,128)S(1)}, f32[4,9,9,128]{3,0,2,1:T(4,128)}, u32[]{:S(2)}) copy-start(f32[4,9,9,128]{3,0,2,1:T(4,128)} %param.21) | copy-start | bytes 497668
  56.1 19.1 %copy-start.14 = (s32[4,128]{1,0:T(4,128)S(1)}, s32[4,128]{1,0:T(4,128)}, u32[]{:S(2)}) copy-start(s32[4,128]{1,0:T(4,128)} %source.1) | copy-start | bytes 6148
  56.2 19.1 %copy-start.15 = (s32[128]{0:T(128)S(1)}, s32[128]{0:T(128)}, u32[]{:S(2)}) copy-start(s32[128]{0:T(128)} %param.24) | copy-start | bytes 1540
  68.1 9.4 %collective-permute-start.9 = (f32[8,256]{1,0:T(8,128)S(1)}, f32[8,256]{1,0:T(8,128)S(1)}, u32[]{:S(2)}, u32[]{:S(2)}) collective-permute-start(f32[8,256]{1,0:T(8,128)S(1)} %get-tuple-element.25), channel_id=1, source_target_pairs={{0,32},{32,64},{64,96},{96,128},{128,160},{160,192},{192,224},{224... | collective-permute-start | bytes 24584 | tf_op jit(solution)/shard_map/ppermute | solution.py:517
  68.4 9.1 %collective-permute-start.10 = (f32[8,256]{1,0:T(8,128)S(1)}, f32[8,256]{1,0:T(8,128)S(1)}, u32[]{:S(2)}, u32[]{:S(2)}) collective-permute-start(f32[8,256]{1,0:T(8,128)S(1)} %get-tuple-element.25), channel_id=1, source_target_pairs={{0,224},{32,0},{64,32},{96,64},{128,96},{160,128},{192,160},{224,1... | collective-permute-start | bytes 24584 | tf_op jit(solution)/shard_map/ppermute | solution.py:517
  70.7 6.7 %collective-permute-start.11 = (f32[8,256]{1,0:T(8,128)S(1)}, f32[8,256]{1,0:T(8,128)S(1)}, u32[]{:S(2)}, u32[]{:S(2)}) collective-permute-start(f32[8,256]{1,0:T(8,128)S(1)} %get-tuple-element.25), channel_id=1, source_target_pairs={{0,4},{4,8},{8,12},{12,16},{16,20},{20,24},{24,28},{28,0},{1,5},{5... | collective-permute-start | bytes 24584 | tf_op jit(solution)/shard_map/ppermute | solution.py:517
  75.3 4.3 %collective-permute-start.12 = (f32[8,256]{1,0:T(8,128)S(1)}, f32[8,256]{1,0:T(8,128)S(1)}, u32[]{:S(2)}, u32[]{:S(2)}) collective-permute-start(f32[8,256]{1,0:T(8,128)S(1)} %get-tuple-element.25), channel_id=1, source_target_pairs={{0,28},{4,0},{8,4},{12,8},{16,12},{20,16},{24,20},{28,24},{1,29},{... | collective-permute-start | bytes 24584 | tf_op jit(solution)/shard_map/ppermute | solution.py:517
  (8 other events, 102.5 us)
